TPU v7x, 128 devices: a whole 4x4x4 slice. The times are simulated.
128 devices in a mesh: rep: 64 (over z, y, x), data: 2 (over core).
Axes of the slice: x: 4, y: 4, z: 4, core: 2. Of those that a mesh axis runs over, the one named last changes fastest.
Arguments:
- img_feat: bfloat16 [393216, 768], P(('rep', 'data'))
- txt_feat: bfloat16 [393216, 512], P(('rep', 'data'))
- w_img: bfloat16 [768, 512], replicated
- w_txt: bfloat16 [512, 512], replicated
- log_temp: float32 [], replicated
- logit_bias: float32 [], replicated
Outputs:
- output 1: float32 [], replicated
- output 2: float32 [], replicated
- output 3: float32 [], replicated
- output 4: float32 [768, 512], replicated
- output 5: float32 [512, 512], replicated
All inputs are finite; a program needn't handle non-finite values.
Results may differ from a plain program's by a relative error of at most 0.001.
Values are sent between devices in bfloat16 or wider.
A program may use at most 1 GiB of HBM per device.

v0:
```python
import jax
import jax.numpy as jnp
from jax import lax
from jax.sharding import PartitionSpec as P


def normalize_rows(raw_emb):
    inv_norm = lax.rsqrt(jnp.sum(raw_emb * raw_emb, axis=1, keepdims=True))
    return raw_emb * inv_norm, inv_norm


def backward_norm(grad_unit, unit_emb, inv_norm):
    proj = jnp.sum(unit_emb * grad_unit, axis=1, keepdims=True)
    return (inv_norm * (grad_unit - unit_emb * proj)).astype(jnp.bfloat16)


def contract_rows(left, right):
    return lax.dot_general(left, right, (((0,), (0,)), ((), ())), preferred_element_type=jnp.float32)


def tile_terms(img_emb, txt_blk, temp_scale, logit_bias, row_offset, total_rows):
    tile_dots = lax.dot_general(img_emb, txt_blk, (((1,), (1,)), ((), ())), preferred_element_type=jnp.float32)
    row_ids = row_offset + jnp.arange(img_emb.shape[0])[:, None]
    col_ids = jnp.arange(txt_blk.shape[0])[None, :]
    sign_mat = jnp.where(row_ids == col_ids, 1.0, -1.0)
    margin = sign_mat * (temp_scale * tile_dots + logit_bias)
    grad_z = -sign_mat * jax.nn.sigmoid(-margin) / total_rows
    scal_part = jnp.stack([jnp.sum(jax.nn.softplus(-margin)), temp_scale * jnp.sum(grad_z * tile_dots), jnp.sum(grad_z)])
    h_mat = (temp_scale * grad_z).astype(jnp.bfloat16)
    img_part = jnp.dot(h_mat, txt_blk, preferred_element_type=jnp.float32)
    txt_part = contract_rows(h_mat, img_emb)
    return img_part, txt_part, scal_part


def solution(mesh):
    data_n = mesh.shape['data']
    rep_n = mesh.shape['rep']
    shift_perm = [(src_dev, (src_dev + 1) % data_n) for src_dev in range(data_n)]
    row_spec = P(('rep', 'data'), None)

    def device_body(img_loc, txt_loc, w_img, w_txt, log_temp, logit_bias):
        rows_n = img_loc.shape[0]
        total_rows = rows_n * rep_n * data_n
        temp_scale = jnp.exp(log_temp)
        unit_img, inv_img = normalize_rows(jnp.dot(img_loc, w_img, preferred_element_type=jnp.float32))
        unit_txt, inv_txt = normalize_rows(jnp.dot(txt_loc, w_txt, preferred_element_type=jnp.float32))
        emb_img = unit_img.astype(jnp.bfloat16)
        emb_txt = unit_txt.astype(jnp.bfloat16)
        home_img, home_txt, home_scal = tile_terms(emb_img, emb_txt, temp_scale, logit_bias, 0, total_rows)

        def visit_step(step_idx, loop_state):
            txt_blk, txt_acc, img_acc, scal_acc = loop_state
            txt_blk = lax.ppermute(txt_blk, 'data', shift_perm)
            txt_acc = lax.ppermute(txt_acc, 'data', shift_perm)
            img_part, txt_part, scal_part = tile_terms(emb_img, txt_blk, temp_scale, logit_bias, rows_n, total_rows)
            return (txt_blk, txt_acc + txt_part, img_acc + img_part, scal_acc + scal_part)

        final_state = lax.fori_loop(1, data_n, visit_step, (emb_txt, home_txt, home_img, home_scal))
        txt_grad = lax.ppermute(final_state[1], 'data', shift_perm)
        img_grad = final_state[2]
        dw_img = contract_rows(img_loc, backward_norm(img_grad, unit_img, inv_img))
        dw_txt = contract_rows(txt_loc, backward_norm(txt_grad, unit_txt, inv_txt))
        dw_img, dw_txt, scal_sum = lax.psum((dw_img, dw_txt, final_state[3]), ('rep', 'data'))
        return scal_sum[0] / total_rows, scal_sum[1], scal_sum[2], dw_img, dw_txt

    return jax.shard_map(device_body, mesh=mesh, in_specs=(row_spec, row_spec, P(), P(), P(), P()), out_specs=(P(), P(), P(), P(), P()), check_vma=False)
```

profile of v0, /device:TPU:1, one launch (start us, length us, event | category | flops | bytes accessed | tf_op | source)
XLA Modules:
  0.0 416.6 jit_solution(6662771324979361638)
XLA Ops:
  7.2 0.0 copy-start
  7.2 0.0 all-reduce.3.cloned.1.call-start
  7.2 1.8 copy-done
  9.1 2.9 multiply_reduce_fusion.6
  12.0 2.7 copy-done.1
  14.8 2.4 multiply_convert_fusion.8
  17.2 1.5 collective-permute-start
  20.0 4.9 %multiply_reduce_fusion.7 = (f32[3072]{0:T(1024)S(1)}, f32[3072,512]{0,1:T(8,128)S(1)}) fusion(bf16[3072,768]{1,0:T(8,128)(2,1)} %param.6, bf16[768,512]{1,0:T(8,128)(2,1)} %param.8), kind=kOutput, calls=%fused_computation.27 | convolution fusion | flops 2419061760 | bytes 11808768 | tf_op jit(solution)/shard_map/dot_general | solution.py:45
  24.9 0.0 copy-start.6
  24.9 2.6 copy-done.2
  27.5 0.0 copy-done.6
  27.5 2.6 multiply_convert_fusion.9
  30.1 56.2 %fusion.2 = (f32[]{:T(128)}, f32[]{:T(128)}, f32[]{:T(128)}, f32[3072,3072]{1,0:T(8,128)}) fusion(f32[]{:T(128)S(6)} %copy.20, f32[]{:T(128)S(6)} %exp.18, bf16[3072,512]{0,1:T(8,128)(2,1)} %multiply_convert_fusion.9, bf16[3072,512]{0,1:T(8,128)(2,1)} %multiply_convert_fusion.8), kind=kOutput, calls=%fused_computation.8 | convolution fusion | flops 9861857280 | bytes 44040212 | tf_op jit(solution)/shard_map/dot_general | solution.py:22
  86.3 19.5 %fusion.4 = f32[3072,512]{0,1:T(8,128)} fusion(bf16[3072,512]{0,1:T(8,128)(2,1)} %multiply_convert_fusion.9, f32[3072,3072]{1,0:T(8,128)} %get-tuple-element.43, f32[]{:T(128)S(6)} %mul.126), kind=kOutput, calls=%fused_computation.18 | convolution fusion | flops 9682550784 | bytes 47185924 | tf_op jit(solution)/shard_map/dot_general | solution.py:18
  105.8 0.0 collective-permute-start.1
  105.9 56.0 %fusion.3 = (f32[]{:T(128)}, f32[]{:T(128)}, f32[]{:T(128)}, f32[3072,3072]{1,0:T(8,128)}) fusion(s32[3072]{0:T(1024)S(1)} %iota_add_fusion, f32[]{:T(128)S(6)} %copy.20, f32[]{:T(128)S(6)} %exp.18, bf16[3072,512]{0,1:T(8,128)(2,1)} %multiply_convert_fusion.9, bf16[3072,512]{0,1:T(8,128)(2,1)} %collective-permute-done), kind=kOutput, calls=%fused_computation.9 | convolution fusion | flops 9861857280 | bytes 44052500 | tf_op jit(solution)/shard_map/while/body/eval_jaxpr/dot_general | solution.py:22
  161.9 0.0 collective-permute-done.1
  161.9 20.2 %fusion.9 = f32[3072,512]{0,1:T(8,128)} fusion(f32[3072,512]{0,1:T(8,128)S(1)} %collective-permute-done.1, bf16[3072,512]{0,1:T(8,128)(2,1)S(1)} %copy-done.3, f32[3072,3072]{1,0:T(8,128)} %get-tuple-element.42, f32[]{:T(128)S(6)} %mul.126), kind=kOutput, calls=%fused_computation.31 | convolution fusion | flops 9684123648 | bytes 53477380 | tf_op jit(solution)/shard_map/while/body/eval_jaxpr/dot_general | solution.py:18
  182.1 0.0 copy-start.7
  182.1 0.6 collective-permute-start.2
  182.7 19.4 %fusion.5 = f32[3072,512]{0,1:T(8,128)} fusion(bf16[3072,512]{0,1:T(8,128)(2,1)} %multiply_convert_fusion.8, f32[3072,3072]{1,0:T(8,128)} %get-tuple-element.43, f32[]{:T(128)S(6)} %mul.126), kind=kOutput, calls=%fused_computation.19 | convolution fusion | flops 9682550784 | bytes 47185924 | tf_op jit(solution)/shard_map/dot_general | solution.py:30
  202.1 23.4 %multiply_reduce_fusion.5 = (f32[3072]{0:T(1024)S(1)}, f32[3072,512]{0,1:T(8,128)}) fusion(f32[3072,512]{0,1:T(8,128)} %copy-done.2, f32[3072]{0:T(1024)S(1)} %copy-done.7, f32[3072,512]{0,1:T(8,128)} %fusion.5, bf16[3072,512]{0,1:T(8,128)(2,1)} %collective-permute-done, f32[3072,3072]{1,0:T(8,128)} %get-tuple-element.42, f32[]{:T(128)S(6)} %mul.126), kind=kOutput, calls=%fused_computation.25 | convolution fusion | flops 9688839168 | bytes 59793412 | tf_op jit(solution)/shard_map/while/body/eval_jaxpr/dot_general | solution.py:30
  225.6 8.7 %fusion.16 = f32[768,512]{0,1:T(8,128)} fusion(bf16[3072,768]{1,0:T(8,128)(2,1)S(1)} %copy-done.8, f32[3072,512]{0,1:T(8,128)} %get-tuple-element.52, f32[3072,512]{0,1:T(8,128)} %copy-done.2, f32[3072]{0:T(1024)S(1)} %get-tuple-element.51, f32[3072]{0:T(1024)S(1)} %copy-done.7), kind=kOutput, calls=%fused_computation.38 | convolution fusion | flops 2423783424 | bytes 18898944 | tf_op jit(solution)/shard_map/dot_general | solution.py:18
  234.3 5.7 %multiply_reduce_fusion.4 = f32[3072]{0:T(1024)S(1)} fusion(f32[3072,512]{0,1:T(8,128)} %collective-permute-done.2, f32[3072,512]{0,1:T(8,128)} %copy-done.1, f32[3072]{0:T(1024)S(1)} %copy-done.5), kind=kLoop, calls=%fused_computation.23 | loop fusion | flops 4715520 | bytes 12607488 | tf_op jit(solution)/shard_map/reduce_sum | solution.py:13
  240.1 7.4 %fusion.17 = f32[512,512]{0,1:T(8,128)} fusion(bf16[3072,512]{1,0:T(8,128)(2,1)S(1)} %copy-done, f32[3072,512]{0,1:T(8,128)} %collective-permute-done.2, f32[3072,512]{0,1:T(8,128)} %copy-done.1, f32[3072]{0:T(1024)S(1)} %multiply_reduce_fusion.4, f32[3072]{0:T(1024)S(1)} %copy-done.5), kind=kOutput, calls=%fused_computation.39 | convolution fusion | flops 1618477056 | bytes 16801792 | tf_op jit(solution)/shard_map/dot_general | solution.py:18
  247.4 0.0 all-reduce.3.cloned.1.call-update
  248.7 2.7 maximum_add_fusion
  251.4 68.7 %psum.21 = f32[3]{0:T(128)S(1)} all-reduce(f32[3]{0:T(128)S(1)} %maximum_add_fusion), channel_id=1, replica_groups=mesh['rep'=64,'data'=2] {'rep','data'}, use_global_device_ids=true, to_apply=%region_8.9 | all-reduce | flops 3 | bytes 24 | tf_op jit(solution)/shard_map/psum | solution.py:63
  320.1 0.6 fusion.20
  321.4 81.5 %all-reduce.3.cloned.1.call-done = (f32[768,512]{0,1:T(8,128)}, f32[512,512]{0,1:T(8,128)}) async-done(((f32[768,512]{0,1:T(8,128)}, f32[512,512]{0,1:T(8,128)}), (f32[768,512]{0,1:T(8,128)}, f32[512,512]{0,1:T(8,128)})) %all-reduce.3.cloned.1.call-update) | async-done | bytes 2621456 | tf_op jit(solution)/shard_map/psum | solution.py:63
  402.9 3.0 copy.13
  405.9 2.5 copy.14
  (16 shorter events, 0.0 us)
Async XLA Ops:
  7.2 1.9 copy-start
  7.2 395.7 %all-reduce.3.cloned.1.call-start = ((), (), s32[]{:S(2)}) async-start(), calls=%async_computation | async-start | bytes 5242880 | tf_op jit(solution)/shard_map/psum | solution.py:63
  12.0 2.8 copy-start.1
  12.0 5.1 %copy-start.4 = (f32[3072]{0:T(1024)}, f32[3072]{0:T(1024)S(1)}, u32[]{:S(2)}) copy-start(f32[3072]{0:T(1024)S(1)} %rsqrt.17) | copy-start | bytes 36868
  17.2 88.7 %collective-permute-start = (bf16[3072,512]{0,1:T(8,128)(2,1)}, bf16[3072,512]{0,1:T(8,128)(2,1)}, u32[]{:S(2)}, u32[]{:S(2)}) collective-permute-start(bf16[3072,512]{0,1:T(8,128)(2,1)} %multiply_convert_fusion.8), channel_id=1, source_target_pairs={{0,1},{1,0},{2,3},{3,2},{4,5},{5,4},{6,7},{7,6},{8,9},{9,8},{10,11... | collective-permute-start | bytes 9437192 | tf_op jit(solution)/shard_map/while/body/eval_jaxpr/ppermute | solution.py:53
  24.9 2.6 copy-start.2
  24.9 2.6 copy-start.6
  105.8 56.1 %collective-permute-start.1 = (f32[3072,512]{0,1:T(8,128)}, f32[3072,512]{0,1:T(8,128)S(1)}, u32[]{:S(2)}, u32[]{:S(2)}) collective-permute-start(f32[3072,512]{0,1:T(8,128)} %fusion.4), channel_id=1, source_target_pairs={{0,1},{1,0},{2,3},{3,2},{4,5},{5,4},{6,7},{7,6},{8,9},{9,8},{10,11... | collective-permute-start | bytes 18874376 | tf_op jit(solution)/shard_map/while/body/eval_jaxpr/ppermute | solution.py:54
  105.8 56.1 %copy-start.3 = (bf16[3072,512]{0,1:T(8,128)(2,1)S(1)}, bf16[3072,512]{0,1:T(8,128)(2,1)}, u32[]{:S(2)}) copy-start(bf16[3072,512]{0,1:T(8,128)(2,1)} %multiply_convert_fusion.9) | copy-start | bytes 9437188
  182.1 20.0 %copy-start.7 = (f32[3072]{0:T(1024)S(1)}, f32[3072]{0:T(1024)}, u32[]{:S(2)}) copy-start(f32[3072]{0:T(1024)} %copy-done.6) | copy-start | bytes 36868
  182.1 52.2 %collective-permute-start.2 = (f32[3072,512]{0,1:T(8,128)}, f32[3072,512]{0,1:T(8,128)}, u32[]{:S(2)}, u32[]{:S(2)}) collective-permute-start(f32[3072,512]{0,1:T(8,128)} %fusion.9), channel_id=1, source_target_pairs={{0,1},{1,0},{2,3},{3,2},{4,5},{5,4},{6,7},{7,6},{8,9},{9,8},{10,11... | collective-permute-start | bytes 18874376 | tf_op jit(solution)/shard_map/ppermute | solution.py:59
  202.1 23.4 %copy-start.8 = (bf16[3072,768]{1,0:T(8,128)(2,1)S(1)}, bf16[3072,768]{1,0:T(8,128)(2,1)}, u32[]{:S(2)}) copy-start(bf16[3072,768]{1,0:T(8,128)(2,1)} %param.6) | copy-start | bytes 14155780
  225.6 8.8 %copy-start.5 = (f32[3072]{0:T(1024)S(1)}, f32[3072]{0:T(1024)}, u32[]{:S(2)}) copy-start(f32[3072]{0:T(1024)} %copy-done.4) | copy-start | bytes 36868
Sparse Core Ops, SparseCore 0:
  247.6 155.2 all-reduce.2
where the time goes:
time: 420 us; the launch traced here: 417 us
  matrix products  219 us (52%)
  waiting for transfers between devices  81.5 us (19%)
  blocking collectives  68.7 us (16%)
  between operations  18.7 us (4%)
  local copies, waits for them, and re-layouts  13.4 us (3%)
  other arithmetic  13.4 us (3%)
    dot_general x2, matrix products, tile_terms(): lax.dot_general(img_emb, txt_blk, (((1,), (1,)), ((), ())), preferred_ele...  112 us
    psum x1, waiting for transfers between devices, device_body(): lax.psum((dw_img, dw_txt, final_state[3]), ('rep', 'data'))  81.5 us
    psum x1, blocking collectives, device_body(): lax.psum((dw_img, dw_txt, final_state[3]), ('rep', 'data'))  68.7 us
    dot_general x4, matrix products, contract_rows(): lax.dot_general(left, right, (((0,), (0,)), ((), ())), preferred_element_...  55.9 us
    dot_general x2, matrix products, tile_terms(): img_part = jnp.dot(h_mat, txt_blk, preferred_element_type=jnp.float32)  42.8 us
    unnamed x20, local copies, waits for them, and re-layouts  12.8 us
  transfers between devices with their start and end apart: 4, of which 1 were waited for; matrix products, arithmetic and copies ran while one was open for 47% of the time, Pallas kernels for 0%

commit v1 on v0

v1 whole, which is shorter than its diff:
```python
import functools

import jax
import jax.numpy as jnp
from jax import lax
from jax.experimental import pallas as pl
from jax.experimental.pallas import tpu as pltpu
from jax.sharding import PartitionSpec as P

LOG2E = 1.4426950408889634
LN2 = 0.6931471805599453
NT = (((1,), (1,)), ((), ()))
TN = (((0,), (0,)), ((), ()))
MESH = pl.DeviceIdType.MESH
F32 = jnp.float32
BF16 = jnp.bfloat16
MIB = 1024 * 1024

BM = 512
BN = 512
CR, CC = 16, 256
HALF = 2688
PART = HALF // 3
QUART = PART // 4
SIXT = QUART // 4


def inv_norm(raw):
    return lax.rsqrt(jnp.sum(raw * raw, axis=1, keepdims=True))


def params(vmem, **kw):
    return pltpu.CompilerParams(dimension_semantics=("arbitrary",), vmem_limit_bytes=vmem * MIB, **kw)


def cost(flops, nbytes):
    return pl.CostEstimate(flops=int(flops), bytes_accessed=int(nbytes), transcendentals=0)


def head_body(x_ref, w_ref, raw_ref, emb_ref, *maybe_t):
    raw = jnp.dot(x_ref[...], w_ref[...], preferred_element_type=F32)
    raw_ref[...] = raw
    emb = (raw * inv_norm(raw)).astype(BF16)
    emb_ref[...] = emb
    if maybe_t:
        maybe_t[0][...] = emb.T


def head(x, w, transposed, name):
    rows, feat = x.shape
    dim = w.shape[1]
    out_shape = [jax.ShapeDtypeStruct((rows, dim), F32), jax.ShapeDtypeStruct((rows, dim), BF16)]
    out_specs = [pl.BlockSpec((BM, dim), lambda i: (i, 0)), pl.BlockSpec((BM, dim), lambda i: (i, 0))]
    if transposed:
        out_shape.append(jax.ShapeDtypeStruct((dim, rows), BF16))
        out_specs.append(pl.BlockSpec((dim, BM), lambda i: (0, i)))
    return pl.pallas_call(
        head_body,
        grid=(rows // BM,),
        in_specs=[pl.BlockSpec((BM, feat), lambda i: (i, 0)), pl.BlockSpec((feat, dim), lambda i: (0, 0))],
        out_specs=out_specs,
        out_shape=out_shape,
        compiler_params=params(24),
        cost_estimate=cost(2 * rows * feat * dim, rows * (2 * feat + 8 * dim)),
        name=name,
    )(x, w)


def pair_terms(sc_ref, img_ref, imgt_ref, txt_ref, di_ref, dt_ref, acc, s_scr, h_scr, total_rows, home, di_init):
    step = pl.program_id(0)
    blocks = txt_ref.shape[0]
    s = sc_ref[0]
    a, b, hs = s * LOG2E, sc_ref[1] * LOG2E, s / total_rows
    img, imgt = img_ref[...], imgt_ref[...]

    def block_of(k):
        return lax.rem(step + k, blocks) if home else k

    def logits(k):
        s_scr[k % 2] = lax.dot_general(img, txt_ref[block_of(k)], NT, preferred_element_type=F32)

    def terms(k):
        zero = jnp.zeros((CR, CC), F32)
        top, prod, g_sum, gs_sum = zero, zero, zero, zero
        for r in range(0, BM, CR):
            for c in range(0, BN, CC):
                dots = s_scr[k % 2, r:r + CR, c:c + CC]
                z = dots * a + b
                pos = jnp.maximum(z, 0.0)
                t = jnp.exp2(-jnp.abs(z))
                rcp = 1.0 / (1.0 + t)
                sig = jnp.where(z >= 0, rcp, t * rcp)
                if home and k == 0 and r < c + CC and c < r + CR:
                    eye = (lax.broadcasted_iota(jnp.int32, (CR, CC), 0) + r) == (lax.broadcasted_iota(jnp.int32, (CR, CC), 1) + c)
                    sig = jnp.where(eye, -jnp.where(z >= 0, t * rcp, rcp), sig)
                    pos = jnp.where(eye, jnp.maximum(-z, 0.0), pos)
                top = top + pos
                prod = (prod + t) + prod * t
                g_sum = g_sum + sig
                gs_sum = gs_sum + sig * dots
                h_scr[k % 2, r:r + CR, c:c + CC] = (sig * hs).astype(BF16)
        acc[0] += LN2 * top + jnp.log1p(prod)
        acc[1] += gs_sum
        acc[2] += g_sum

    def grads(k):
        h = h_scr[k % 2]
        part = jnp.dot(h, txt_ref[block_of(k)], preferred_element_type=F32)
        if k == 0:
            di_ref[...] = part if di_init is None else di_init[...] + part
        else:
            di_ref[...] += part
        dt_ref[block_of(k)] += jnp.dot(imgt, h, preferred_element_type=F32)

    logits(0)
    for k in range(blocks):
        if k + 1 < blocks:
            logits(k + 1)
        terms(k)
        grads(k)


def away_body(sc_ref, img_ref, imgt_ref, txt_ref, di_ref, dt_ref, sums_ref, s_scr, h_scr, *, total_rows):
    @pl.when(pl.program_id(0) == 0)
    def _():
        sums_ref[...] = jnp.zeros_like(sums_ref)
        dt_ref[...] = jnp.zeros_like(dt_ref)

    pair_terms(sc_ref, img_ref, imgt_ref, txt_ref, di_ref, dt_ref, sums_ref, s_scr, h_scr, total_rows, False, None)


def home_body(sc_ref, img_ref, imgt_ref, txt_ref, raw_ref, x_ref, away_ref, sums_in, dt_ref, dw_ref, sums_ref, s_scr, h_scr, di_ref, *, total_rows):
    @pl.when(pl.program_id(0) == 0)
    def _():
        sums_ref[...] = sums_in[...]
        dt_ref[...] = jnp.zeros_like(dt_ref)
        dw_ref[...] = jnp.zeros_like(dw_ref)

    pair_terms(sc_ref, img_ref, imgt_ref, txt_ref, di_ref, dt_ref, sums_ref, s_scr, h_scr, total_rows, True, away_ref)
    dw_ref[...] += lax.dot_general(x_ref[...], raw_grad(raw_ref[...], di_ref[...]), TN, preferred_element_type=F32)


def raw_grad(raw, grad_unit):
    inv = inv_norm(raw)
    unit = raw * inv
    proj = jnp.sum(unit * grad_unit, axis=1, keepdims=True)
    return (inv * (grad_unit - unit * proj)).astype(BF16)


def tile_scratch():
    return [pltpu.VMEM((2, BM, BN), F32), pltpu.VMEM((2, BM, BN), BF16)]


def whole(shape, **kw):
    return pl.BlockSpec(shape, lambda i: (0,) * len(shape), **kw)


def away_tile(scal, img, imgt, txt, total_rows):
    rows, dim = img.shape
    blocks = txt.shape[0]
    once = dict(pipeline_mode=pl.Buffered(1))
    return pl.pallas_call(
        functools.partial(away_body, total_rows=total_rows),
        grid=(rows // BM,),
        in_specs=[
            pl.BlockSpec(memory_space=pltpu.SMEM),
            pl.BlockSpec((BM, dim), lambda i: (i, 0)),
            pl.BlockSpec((dim, BM), lambda i: (0, i)),
            whole((blocks, BN, dim), **once),
        ],
        out_specs=[pl.BlockSpec((BM, dim), lambda i: (i, 0)), whole((blocks, dim, BN), **once), whole((3, CR, CC))],
        out_shape=[
            jax.ShapeDtypeStruct((rows, dim), F32),
            jax.ShapeDtypeStruct((blocks, dim, BN), F32),
            jax.ShapeDtypeStruct((3, CR, CC), F32),
        ],
        scratch_shapes=tile_scratch(),
        compiler_params=params(40),
        cost_estimate=cost(6 * rows * rows * dim, 30 * rows * dim),
        name="away_tile",
    )(scal, img, imgt, txt)


def home_tile(scal, img, imgt, txt, raw, x, away, sums, total_rows):
    rows, dim = img.shape
    feat = x.shape[1]
    blocks = txt.shape[0]
    once = dict(pipeline_mode=pl.Buffered(1))
    return pl.pallas_call(
        functools.partial(home_body, total_rows=total_rows),
        grid=(rows // BM,),
        in_specs=[
            pl.BlockSpec(memory_space=pltpu.SMEM),
            pl.BlockSpec((BM, dim), lambda i: (i, 0)),
            pl.BlockSpec((dim, BM), lambda i: (0, i)),
            whole((blocks, BN, dim), **once),
            pl.BlockSpec((BM, dim), lambda i: (i, 0)),
            pl.BlockSpec((BM, feat), lambda i: (i, 0)),
            pl.BlockSpec((BM, dim), lambda i: (i, 0)),
            whole((3, CR, CC)),
        ],
        out_specs=[whole((blocks, dim, BN), **once), whole((feat, dim), **once), whole((3, CR, CC))],
        out_shape=[
            jax.ShapeDtypeStruct((blocks, dim, BN), F32),
            jax.ShapeDtypeStruct((feat, dim), F32),
            jax.ShapeDtypeStruct((3, CR, CC), F32),
        ],
        scratch_shapes=tile_scratch() + [pltpu.VMEM((BM, dim), F32)],
        compiler_params=params(48),
        cost_estimate=cost(6 * rows * rows * dim, 40 * rows * dim),
        name="home_tile",
    )(scal, img, imgt, txt, raw, x, away, sums)


def text_body(sc_ref, own_ref, got_ref, raw_ref, x_ref, dwi_ref, sums_ref, out_ref, dw_ref, *, total_rows):
    step = pl.program_id(0)

    @pl.when(step == 0)
    def _():
        dw_ref[...] = jnp.zeros_like(dw_ref)

    grad = (own_ref[0] + got_ref[0]).T
    dw_ref[...] += lax.dot_general(x_ref[...], raw_grad(raw_ref[...], grad), TN, preferred_element_type=F32)

    @pl.when(step == pl.num_programs(0) - 1)
    def _():
        feat_i, feat_t = dwi_ref.shape[0], dw_ref.shape[0]
        flat = []
        for l in range(4):
            flat.append((dwi_ref, l, feat_i))
        for l in range(4):
            flat.append((dw_ref, l, feat_t))
        pos = 0
        size = 2 * feat_i + 2 * feat_t
        for ref, l, n in flat:
            done = 0
            while done < n:
                half, at = divmod(pos, size)
                take = min(n - done, size - at)
                out_ref[half, at:at + take, :] = ref[done:done + take, 128 * l:128 * (l + 1)]
                done += take
                pos += take
        out_ref[:, size:, :] = jnp.zeros((2, HALF - size, 128), F32)
        s = sc_ref[0]
        row = lax.broadcasted_iota(jnp.int32, (8, 128), 0)
        loss = jnp.sum(sums_ref[0]) / total_rows
        temp = jnp.sum(sums_ref[1]) * (s / total_rows)
        bias = jnp.sum(sums_ref[2]) / total_rows
        out_ref[0, size:size + 8, :] = jnp.where(row == 0, loss, jnp.where(row == 1, temp, bias))


def text_back(scal, own, got, raw, x, dwi, sums, total_rows):
    rows, dim = raw.shape
    feat = x.shape[1]
    return pl.pallas_call(
        functools.partial(text_body, total_rows=total_rows),
        grid=(rows // BN,),
        in_specs=[
            pl.BlockSpec(memory_space=pltpu.SMEM),
            pl.BlockSpec((1, dim, BN), lambda i: (i, 0, 0)),
            pl.BlockSpec((1, dim, BN), lambda i: (i, 0, 0)),
            pl.BlockSpec((BN, dim), lambda i: (i, 0)),
            pl.BlockSpec((BN, feat), lambda i: (i, 0)),
            whole(dwi.shape),
            whole((3, CR, CC)),
        ],
        out_specs=whole((2, HALF, 128)),
        out_shape=jax.ShapeDtypeStruct((2, HALF, 128), F32),
        scratch_shapes=[pltpu.VMEM((feat, dim), F32)],
        compiler_params=params(32),
        cost_estimate=cost(2 * rows * feat * dim, rows * (2 * feat + 12 * dim)),
        name="text_back",
    )(scal, own, got, raw, x, dwi, sums)


def allsum_body(a_ref, o_ref, d2d, r1, r2, r3, dsem, s1, v1, s2, v2, s3, v3, s4, v4, s5, v5):
    rep, core = lax.axis_index("rep"), lax.axis_index("data")
    coord = [lax.rem(rep, 4), lax.rem(lax.div(rep, 4), 4), lax.div(rep, 16)]
    stride = [1, 4, 16]

    def peer(dim, off):
        return (rep + (lax.rem(coord[dim] + off, 4) - coord[dim]) * stride[dim], core)

    sib = (rep, 1 - core)
    bar = pltpu.get_barrier_semaphore()
    pl.semaphore_signal(bar, inc=1, device_id=sib, device_id_type=MESH)
    for dim in range(3):
        for off in (1, 2, 3):
            pl.semaphore_signal(bar, inc=1, device_id=peer(dim, off), device_id_type=MESH)
    pl.semaphore_wait(bar, 10)

    started = []

    def send(src, dst, ssem, rsem, dev):
        copy = pltpu.make_async_remote_copy(src_ref=src, dst_ref=dst, send_sem=ssem, recv_sem=rsem, device_id=dev, device_id_type=MESH)
        copy.start()
        started.append(copy)
        return copy

    out = o_ref.at[core]
    dims = [(p, (p + 1) % 3, (p + 2) % 3) for p in range(3)]
    offs = (2, 1, 3)

    c0 = []
    for p in range(3):
        rows = pl.ds(PART * p, PART)
        c0.append(send(a_ref.at[1 - core, rows], d2d.at[rows], dsem.at[0, p], dsem.at[1, p], sib))
    c1 = []
    for p in range(3):
        c0[p].wait_recv()
        rows = pl.ds(PART * p, PART)
        d2d[rows, :] = d2d[rows, :] + a_ref[core, rows, :]
        d = dims[p][0]
        c1.append([
            send(d2d.at[pl.ds(PART * p + lax.rem(coord[d] + o, 4) * QUART, QUART)], r1.at[p, o - 1], s1.at[p, o - 1], v1.at[p, o - 1], peer(d, o))
            for o in offs
        ])
    c2, base1 = [], []
    for p in range(3):
        for copy in c1[p]:
            copy.wait_recv()
        base = PART * p + coord[dims[p][0]] * QUART
        base1.append(base)
        mine = pl.ds(base, QUART)
        d2d[mine, :] = ((d2d[mine, :] + r1[p, 0]) + r1[p, 1]) + r1[p, 2]
        d = dims[p][1]
        c2.append([
            send(d2d.at[pl.ds(base + lax.rem(coord[d] + o, 4) * SIXT, SIXT)], r2.at[p, o - 1], s2.at[p, o - 1], v2.at[p, o - 1], peer(d, o))
            for o in offs
        ])
    c3, base2 = [], []
    for p in range(3):
        for copy in c2[p]:
            copy.wait_recv()
        base = base1[p] + coord[dims[p][1]] * SIXT
        base2.append(base)
        d = dims[p][2]
        k = coord[d]
        r3[p, k] = ((d2d[pl.ds(base, SIXT), :] + r2[p, 0]) + r2[p, 1]) + r2[p, 2]
        c3.append([send(r3.at[p, k], r3.at[p, k], s3.at[p, o - 1], v3.at[p, o - 1], peer(d, o)) for o in offs])
    c4 = []
    for p in range(3):
        for copy in c3[p]:
            copy.wait_recv()
        mine = pl.ds(base2[p], SIXT)
        o_ref[core, mine, :] = ((r3[p, 0] + r3[p, 1]) + r3[p, 2]) + r3[p, 3]
        c4.append([send(out.at[mine], out.at[mine], s4.at[p, o - 1], v4.at[p, o - 1], peer(dims[p][1], o)) for o in offs])
    c5, c6 = [], []
    for p in range(3):
        for copy in c4[p]:
            copy.wait_recv()
        mine = pl.ds(base1[p], QUART)
        c5.append([send(out.at[mine], out.at[mine], s5.at[p, o - 1], v5.at[p, o - 1], peer(dims[p][0], o)) for o in offs])
        c6.append(send(out.at[mine], out.at[mine], dsem.at[2, p], dsem.at[3, p], sib))
    for p in range(3):
        for i, o in enumerate(offs):
            c5[p][i].wait_recv()
            src = pl.ds(PART * p + lax.rem(coord[dims[p][0]] + 4 - o, 4) * QUART, QUART)
            c6.append(send(out.at[src], out.at[src], dsem.at[4 + 2 * i, p], dsem.at[5 + 2 * i, p], sib))
    for copy in c6:
        copy.wait_recv()
    for copy in started:
        copy.wait_send()


def allsum(packed):
    dma = pltpu.SemaphoreType.DMA
    return pl.pallas_call(
        allsum_body,
        in_specs=[pl.BlockSpec(memory_space=pltpu.VMEM)],
        out_specs=pl.BlockSpec(memory_space=pltpu.VMEM),
        out_shape=jax.ShapeDtypeStruct((2, HALF, 128), F32),
        scratch_shapes=[
            pltpu.VMEM((HALF, 128), F32),
            pltpu.VMEM((3, 3, QUART, 128), F32),
            pltpu.VMEM((3, 3, SIXT, 128), F32),
            pltpu.VMEM((3, 4, SIXT, 128), F32),
            dma((10, 3)),
        ] + [dma((3, 3)) for _ in range(10)],
        compiler_params=pltpu.CompilerParams(collective_id=1, has_side_effects=True, vmem_limit_bytes=24 * MIB),
        cost_estimate=cost(1e9, 1e7),
        name="allsum",
    )(packed)


def solution(mesh):
    data_n, rep_n = mesh.shape["data"], mesh.shape["rep"]
    swap = [(src, (src + 1) % data_n) for src in range(data_n)]
    row_spec = P(("rep", "data"), None)

    def device_body(img_loc, txt_loc, w_img, w_txt, log_temp, logit_bias):
        rows, feat_i = img_loc.shape
        feat_t = txt_loc.shape[1]
        dim = w_img.shape[1]
        total_rows = float(rows * rep_n * data_n)
        scal = jnp.stack([jnp.exp(log_temp), logit_bias])
        raw_t, emb_t = head(txt_loc, w_txt, False, "text_head")
        emb_t = emb_t.reshape(rows // BN, BN, dim)
        away_t = lax.ppermute(emb_t, "data", swap)
        raw_i, emb_i, emb_it = head(img_loc, w_img, True, "image_head")
        away_di, away_dt, sums = away_tile(scal, emb_i, emb_it, away_t, total_rows)
        got_dt = lax.ppermute(away_dt, "data", swap)
        own_dt, dwi, sums = home_tile(scal, emb_i, emb_it, emb_t, raw_i, img_loc, away_di, sums, total_rows)
        packed = text_back(scal, own_dt, got_dt, raw_t, txt_loc, dwi, sums, total_rows)
        total = allsum(packed)
        size = 2 * (feat_i + feat_t)
        split = 4 * feat_i - size
        flat_i = jnp.concatenate([total[0, :size], total[1, :split]])
        flat_t = total[1, split:size]
        dw_img = flat_i.reshape(4, feat_i, 128).transpose(1, 0, 2).reshape(feat_i, dim)
        dw_txt = flat_t.reshape(4, feat_t, 128).transpose(1, 0, 2).reshape(feat_t, dim)
        return total[0, size, 0], total[0, size + 1, 0], total[0, size + 2, 0], dw_img, dw_txt

    return jax.shard_map(device_body, mesh=mesh, in_specs=(row_spec, row_spec, P(), P(), P(), P()), out_specs=(P(), P(), P(), P(), P()), check_vma=False)
```

time: 420 us -> 172 us (0.41)
  matrix products: 219 us -> 0 us
  Pallas kernels: 0 us -> 148 us
  waiting for transfers between devices: 81.5 us -> 0.01 us
  blocking collectives: 68.7 us -> 0 us
  between operations: 18.7 us -> 2.09 us
  other arithmetic: 13.4 us -> 0.18 us
  local copies, waits for them, and re-layouts: 13.4 us -> 19.5 us
    dot_general x10 -> x0, matrix products: 219 us -> none  [the longest x2 112 us: tile_terms(): lax.dot_general(img_emb, txt_blk, (((1,), (1,)), ((), ())), preferred_ele...]
    pallas_call x0 -> x6, Pallas kernels: none -> 148 us  [the longest x1 48.3 us: home_tile(): pl.pallas_call(functools.partial(home_body, total_rows=total_rows), grid=...]
    psum x1 -> x0, waiting for transfers between devices: 81.5 us -> none  [device_body(): lax.psum((dw_img, dw_txt, final_state[3]), ('rep', 'data'))]
    psum x1 -> x0, blocking collectives: 68.7 us -> none  [device_body(): lax.psum((dw_img, dw_txt, final_state[3]), ('rep', 'data'))]
    reduce_sum x1 -> x0, other arithmetic: 5.71 us -> none  [backward_norm(): proj = jnp.sum(unit_emb * grad_unit, axis=1, keepdims=True)]
    convert_element_type x2 -> x0, other arithmetic: 4.95 us -> none  [the longest x1 2.57 us: device_body(): emb_img = unit_img.astype(jnp.bfloat16)]
    unnamed x20 -> x24, local copies, waits for them, and re-layouts: 12.8 us -> 16.3 us
  transfers between devices with their start and end apart: 4 -> 2, of which waited for: 1 -> 0; matrix products, arithmetic and copies ran while one was open for 47% -> 0% of each run, Pallas kernels for 0% -> 31%
where the time goes in v1:
time: 172 us; the launch traced here: 171 us
  Pallas kernels  148 us (86%)
  local copies, waits for them, and re-layouts  19.5 us (11%)
  between operations  2.09 us (1%)
    pallas_call x1, Pallas kernels, home_tile(): pl.pallas_call(functools.partial(home_body, total_rows=total_rows), grid=...  48.3 us
    pallas_call x1, Pallas kernels, away_tile(): pl.pallas_call(functools.partial(away_body, total_rows=total_rows), grid=...  44.8 us
    pallas_call x1, Pallas kernels, allsum(): pl.pallas_call(allsum_body, in_specs=[pl.BlockSpec(memory_space=pltpu.VME...  37.8 us
    unnamed x24, local copies, waits for them, and re-layouts  16.3 us
    pallas_call x1, Pallas kernels, text_back(): pl.pallas_call(functools.partial(text_body, total_rows=total_rows), grid=...  8.63 us
    pallas_call x2, Pallas kernels, head(): pl.pallas_call(head_body, grid=(rows // BM,), in_specs=[pl.BlockSpec((BM,...  8.31 us
  transfers between devices with their start and end apart: 2, of which 0 were waited for; matrix products, arithmetic and copies ran while one was open for 0% of the time, Pallas kernels for 31%

profile of v1, /device:TPU:1, one launch (start us, length us, event | category | flops | bytes accessed | tf_op | source)
XLA Modules:
  0.0 171.2 jit_solution(16788755616439965044)
XLA Ops:
  0.6 0.0 copy-start.2
  0.6 1.9 %copy-done.2 = bf16[3072,512]{1,0:T(8,128)(2,1)S(1)} copy-done((bf16[3072,512]{1,0:T(8,128)(2,1)S(1)}, bf16[3072,512]{1,0:T(8,128)(2,1)}, u32[]{:S(2)}) %copy-start.2) | copy-done | bytes 3145752
  2.5 1.0 copy-done.7
  3.6 3.2 %text_head.1 = (f32[3072,512]{1,0:T(8,128)S(1)}, bf16[3072,512]{1,0:T(8,128)(2,1)S(1)}) custom-call(bf16[3072,512]{1,0:T(8,128)(2,1)S(1)} %copy-done.2, bf16[512,512]{1,0:T(8,128)(2,1)S(1)} %copy-done.7), custom_call_target="tpu_custom_call" | custom-call | flops 1610612736 | bytes 15728640 | tf_op jit(solution)/shard_map/text_head/pallas_call | solution.py:57
  6.8 0.0 copy-start
  6.8 2.6 %copy-done = f32[3072,512]{1,0:T(8,128)} copy-done((f32[3072,512]{1,0:T(8,128)}, f32[3072,512]{1,0:T(8,128)S(1)}, u32[]{:S(2)}) %copy-start) | copy-done | bytes 6291480
  9.4 1.4 collective-permute-start
  12.1 0.1 pad_maximum_fusion.1.sc_ref
  12.2 2.3 %copy-done.4 = bf16[3072,768]{1,0:T(8,128)(2,1)S(1)} copy-done((bf16[3072,768]{1,0:T(8,128)(2,1)S(1)}, bf16[3072,768]{1,0:T(8,128)(2,1)}, u32[]{:S(2)}) %copy-start.4) | copy-done | bytes 4718616
  14.5 1.1 copy-done.6
  15.7 5.1 %image_head.1 = (f32[3072,512]{1,0:T(8,128)S(1)}, bf16[3072,512]{1,0:T(8,128)(2,1)S(1)}, bf16[512,3072]{1,0:T(8,128)(2,1)S(1)}) custom-call(bf16[3072,768]{1,0:T(8,128)(2,1)S(1)} %copy-done.4, bf16[768,512]{1,0:T(8,128)(2,1)S(1)} %copy-done.6), custom_call_target="tpu_custom_call" | custom-call | flops 2415919104 | bytes 17301504 | tf_op jit(solution)/shard_map/image_head/pallas_call | solution.py:57
  20.8 0.0 copy-done.5
  20.8 0.0 copy-start.8
  20.8 2.6 %copy-done.8 = f32[3072,512]{1,0:T(8,128)} copy-done((f32[3072,512]{1,0:T(8,128)}, f32[3072,512]{1,0:T(8,128)S(1)}, u32[]{:S(2)}) %copy-start.8) | copy-done | bytes 6291480
  23.4 0.0 collective-permute-done.txt_ref
  23.4 44.8 %away_tile.1 = (f32[3072,512]{1,0:T(8,128)}, f32[6,512,512]{2,1,0:T(8,128)}, f32[3,16,256]{2,1,0:T(8,128)S(1)}) custom-call(f32[2]{0:T(128)S(1)} %pad_maximum_fusion.1.sc_ref, bf16[3072,512]{1,0:T(8,128)(2,1)S(1)} %get-tuple-element.16.img_ref, bf16[512,3072]{1,0:T(8,128)(2,1)S(1)} %get-tuple-element.17.imgt_ref, ...), custom_call_target="tpu_custom_call" | custom-call | flops 28991029248 | bytes 47185920 | tf_op jit(solution)/shard_map/away_tile/pallas_call | solution.py:162
  68.2 0.0 copy-done.9
  68.2 0.0 copy-done.11
  68.2 0.3 collective-permute-start.1
  68.5 1.9 %copy-done.10 = bf16[3072,512]{1,0:T(8,128)(2,1)S(1)} copy-done((bf16[3072,512]{1,0:T(8,128)(2,1)S(1)}, bf16[3072,512]{1,0:T(8,128)(2,1)}, u32[]{:S(2)}) %copy-start.10) | copy-done | bytes 3145752
  70.4 48.3 %home_tile.1 = (f32[6,512,512]{2,1,0:T(8,128)}, f32[768,512]{1,0:T(8,128)S(1)}, f32[3,16,256]{2,1,0:T(8,128)S(1)}) custom-call(f32[2]{0:T(128)S(1)} %pad_maximum_fusion.1.sc_ref, bf16[3072,512]{1,0:T(8,128)(2,1)S(1)} %copy-done.10, bf16[512,3072]{1,0:T(8,128)(2,1)} %copy-done.11, bf16[6,512,512]{2,1,0:T(8,128)(2,1)} %bitcast.26, f32[3072,512]{1,0:T(8,128)} %copy-done.8, ...), custom_call_target="tpu_custom_call" | custom-call | flops 28991029248 | bytes 62914560 | tf_op jit(solution)/shard_map/home_tile/pallas_call | solution.py:189
  118.7 0.0 collective-permute-done.1.got_ref
  118.7 0.0 copy-start.1
  118.7 2.8 %copy-done.1 = f32[6,512,512]{2,1,0:T(8,128)S(1)} copy-done((f32[6,512,512]{2,1,0:T(8,128)S(1)}, f32[6,512,512]{2,1,0:T(8,128)}, u32[]{:S(2)}) %copy-start.1) | copy-done | bytes 6291480
  121.5 8.6 %text_back.1.a_ref = f32[2,2688,128]{2,1,0:T(8,128)S(1)} custom-call(f32[2]{0:T(128)S(1)} %pad_maximum_fusion.1.sc_ref, f32[6,512,512]{2,1,0:T(8,128)S(1)} %copy-done.1, f32[6,512,512]{2,1,0:T(8,128)S(1)} %collective-permute-done.1.got_ref, f32[3072,512]{1,0:T(8,128)} %copy-done, bf16[3072,512]{1,0:T(8,128)(2,1)S(1)} %copy-done.3, ...), custom_call_target="tpu_custom_call" | custom-call | flops 1610612736 | bytes 22020096 | tf_op jit(solution)/shard_map/text_back/pallas_call | solution.py:255
  130.1 37.8 %allsum.1 = f32[2,2688,128]{2,1,0:T(8,128)S(1)} custom-call(f32[2,2688,128]{2,1,0:T(8,128)S(1)} %text_back.1.a_ref), custom_call_target="tpu_custom_call" | custom-call | flops 1000000000 | bytes 10000000 | tf_op jit(solution)/shard_map/allsum/pallas_call | solution.py:368
  167.9 0.5 fusion
  168.5 0.1 slice.23
  168.5 0.1 slice_bitcast_fusion
  168.6 0.1 pad_maximum_fusion
  168.7 1.4 copy.17
  170.1 1.1 copy.18
  (10 shorter events, 0.0 us)
Async XLA Ops:
  0.6 1.9 %copy-start.2 = (bf16[3072,512]{1,0:T(8,128)(2,1)S(1)}, bf16[3072,512]{1,0:T(8,128)(2,1)}, u32[]{:S(2)}) copy-start(bf16[3072,512]{1,0:T(8,128)(2,1)} %x_ref.7) | copy-start | bytes 9437188
  2.5 1.0 copy-start.7
  6.8 2.7 %copy-start = (f32[3072,512]{1,0:T(8,128)}, f32[3072,512]{1,0:T(8,128)S(1)}, u32[]{:S(2)}) copy-start(f32[3072,512]{1,0:T(8,128)S(1)} %get-tuple-element.24.raw_ref) | copy-start | bytes 18874372
  9.4 11.4 %copy-start.5 = (bf16[3072,512]{1,0:T(8,128)(2,1)}, bf16[3072,512]{1,0:T(8,128)(2,1)S(1)}, u32[]{:S(2)}) copy-start(bf16[3072,512]{1,0:T(8,128)(2,1)S(1)} %get-tuple-element.18) | copy-start | bytes 9437188
  9.4 14.0 %collective-permute-start = (bf16[6,512,512]{2,1,0:T(8,128)(2,1)S(1)}, bf16[6,512,512]{2,1,0:T(8,128)(2,1)}, u32[]{:S(2)}, u32[]{:S(2)}) collective-permute-start(bf16[6,512,512]{2,1,0:T(8,128)(2,1)S(1)} %bitcast.25), channel_id=1, source_target_pairs={{0,1},{1,0},{2,3},{3,2},{4,5},{5,4},{6,7},{7,6},{8,9},{9,8},{10,11... | collective-permute-start | bytes 9437192 | tf_op jit(solution)/shard_map/ppermute | solution.py:399
  12.2 2.3 %copy-start.4 = (bf16[3072,768]{1,0:T(8,128)(2,1)S(1)}, bf16[3072,768]{1,0:T(8,128)(2,1)}, u32[]{:S(2)}) copy-start(bf16[3072,768]{1,0:T(8,128)(2,1)} %x_ref.6) | copy-start | bytes 14155780
  14.5 1.1 copy-start.6
  20.8 2.6 %copy-start.8 = (f32[3072,512]{1,0:T(8,128)}, f32[3072,512]{1,0:T(8,128)S(1)}, u32[]{:S(2)}) copy-start(f32[3072,512]{1,0:T(8,128)S(1)} %get-tuple-element.19.raw_ref) | copy-start | bytes 18874372
  23.4 44.8 %copy-start.9 = (bf16[3072,512]{1,0:T(8,128)(2,1)}, bf16[3072,512]{1,0:T(8,128)(2,1)S(1)}, u32[]{:S(2)}) copy-start(bf16[3072,512]{1,0:T(8,128)(2,1)S(1)} %get-tuple-element.16.img_ref) | copy-start | bytes 9437188
  23.4 44.8 %copy-start.11 = (bf16[512,3072]{1,0:T(8,128)(2,1)}, bf16[512,3072]{1,0:T(8,128)(2,1)S(1)}, u32[]{:S(2)}) copy-start(bf16[512,3072]{1,0:T(8,128)(2,1)S(1)} %get-tuple-element.17.imgt_ref) | copy-start | bytes 9437188
  68.2 50.5 %collective-permute-start.1 = (f32[6,512,512]{2,1,0:T(8,128)}, f32[6,512,512]{2,1,0:T(8,128)S(1)}, u32[]{:S(2)}, u32[]{:S(2)}) collective-permute-start(f32[6,512,512]{2,1,0:T(8,128)} %get-tuple-element.23), channel_id=1, source_target_pairs={{0,1},{1,0},{2,3},{3,2},{4,5},{5,4},{6,7},{7,6},{8,9},{9,8},{10,11... | collective-permute-start | bytes 18874376 | tf_op jit(solution)/shard_map/ppermute | solution.py:402
  68.5 1.9 %copy-start.10 = (bf16[3072,512]{1,0:T(8,128)(2,1)S(1)}, bf16[3072,512]{1,0:T(8,128)(2,1)}, u32[]{:S(2)}) copy-start(bf16[3072,512]{1,0:T(8,128)(2,1)} %copy-done.9) | copy-start | bytes 9437188
  70.4 48.3 %copy-start.3 = (bf16[3072,512]{1,0:T(8,128)(2,1)S(1)}, bf16[3072,512]{1,0:T(8,128)(2,1)}, u32[]{:S(2)}) copy-start(bf16[3072,512]{1,0:T(8,128)(2,1)} %x_ref.7) | copy-start | bytes 9437188
  118.7 2.8 %copy-start.1 = (f32[6,512,512]{2,1,0:T(8,128)S(1)}, f32[6,512,512]{2,1,0:T(8,128)}, u32[]{:S(2)}) copy-start(f32[6,512,512]{2,1,0:T(8,128)} %get-tuple-element.22.own_ref) | copy-start | bytes 18874372

commit v2 on v1

--- a/solution.py
+++ b/solution.py
@@ -60,7 +60,7 @@
         in_specs=[pl.BlockSpec((BM, feat), lambda i: (i, 0)), pl.BlockSpec((feat, dim), lambda i: (0, 0))],
         out_specs=out_specs,
         out_shape=out_shape,
-        compiler_params=params(24),
+        compiler_params=params(62),
         cost_estimate=cost(2 * rows * feat * dim, rows * (2 * feat + 8 * dim)),
         name=name,
     )(x, w)
@@ -175,7 +175,7 @@
             jax.ShapeDtypeStruct((3, CR, CC), F32),
         ],
         scratch_shapes=tile_scratch(),
-        compiler_params=params(40),
+        compiler_params=params(62),
         cost_estimate=cost(6 * rows * rows * dim, 30 * rows * dim),
         name="away_tile",
     )(scal, img, imgt, txt)
@@ -206,7 +206,7 @@
             jax.ShapeDtypeStruct((3, CR, CC), F32),
         ],
         scratch_shapes=tile_scratch() + [pltpu.VMEM((BM, dim), F32)],
-        compiler_params=params(48),
+        compiler_params=params(62),
         cost_estimate=cost(6 * rows * rows * dim, 40 * rows * dim),
         name="home_tile",
     )(scal, img, imgt, txt, raw, x, away, sums)
@@ -267,7 +267,7 @@
         out_specs=whole((2, HALF, 128)),
         out_shape=jax.ShapeDtypeStruct((2, HALF, 128), F32),
         scratch_shapes=[pltpu.VMEM((feat, dim), F32)],
-        compiler_params=params(32),
+        compiler_params=params(57),
         cost_estimate=cost(2 * rows * feat * dim, rows * (2 * feat + 12 * dim)),
         name="text_back",
     )(scal, own, got, raw, x, dwi, sums)

time: 172 us -> 168 us (0.977)
  local copies, waits for them, and re-layouts: 19.5 us -> 4.94 us
  Pallas kernels: 148 us -> 158 us
    unnamed x24 -> x2, local copies, waits for them, and re-layouts: 16.3 us -> 1.78 us
    pallas_call x2, Pallas kernels: 8.31 us -> 17.5 us  [head(): pl.pallas_call(head_body, grid=(rows // BM,), in_specs=[pl.BlockSpec((BM,...]
    pallas_call x1, Pallas kernels: 8.63 us -> 13.6 us  [text_back(): pl.pallas_call(functools.partial(text_body, total_rows=total_rows), grid=...]
    pallas_call x1, Pallas kernels: 44.8 us -> 42.2 us  [away_tile(): pl.pallas_call(functools.partial(away_body, total_rows=total_rows), grid=...]
  transfers between devices with their start and end apart: 2 -> 2, of which waited for: 0 -> 0; matrix products, arithmetic and copies ran while one was open for 0% -> 0% of each run, Pallas kernels for 31% -> 34%
where the time goes in v2:
time: 168 us; the launch traced here: 167 us
  Pallas kernels  158 us (94%)
  local copies, waits for them, and re-layouts  4.94 us (3%)
  between operations  2.02 us (1%)
    pallas_call x1, Pallas kernels, home_tile(): pl.pallas_call(functools.partial(home_body, total_rows=total_rows), grid=...  47.2 us
    pallas_call x1, Pallas kernels, away_tile(): pl.pallas_call(functools.partial(away_body, total_rows=total_rows), grid=...  42.2 us
    pallas_call x1, Pallas kernels, allsum(): pl.pallas_call(allsum_body, in_specs=[pl.BlockSpec(memory_space=pltpu.VME...  37.5 us
    pallas_call x2, Pallas kernels, head(): pl.pallas_call(head_body, grid=(rows // BM,), in_specs=[pl.BlockSpec((BM,...  17.5 us
    pallas_call x1, Pallas kernels, text_back(): pl.pallas_call(functools.partial(text_body, total_rows=total_rows), grid=...  13.6 us
  transfers between devices with their start and end apart: 2, of which 0 were waited for; matrix products, arithmetic and copies ran while one was open for 0% of the time, Pallas kernels for 34%

profile of v2, /device:TPU:1, one launch (start us, length us, event | category | flops | bytes accessed | tf_op | source)
XLA Modules:
  0.0 167.3 jit_solution(8317231599463415257)
XLA Ops:
  0.6 7.7 %text_head.1 = (f32[3072,512]{1,0:T(8,128)}, bf16[3072,512]{1,0:T(8,128)(2,1)}) custom-call(bf16[3072,512]{1,0:T(8,128)(2,1)} %x_ref.7, bf16[512,512]{1,0:T(8,128)(2,1)} %w_ref.3), custom_call_target="tpu_custom_call" | custom-call | flops 1610612736 | bytes 15728640 | tf_op jit(solution)/shard_map/text_head/pallas_call | solution.py:57
  8.4 1.4 collective-permute-start
  11.1 0.6 pad_maximum_fusion.1.sc_ref
  11.6 9.7 %image_head.1 = (f32[3072,512]{1,0:T(8,128)}, bf16[3072,512]{1,0:T(8,128)(2,1)}, bf16[512,3072]{1,0:T(8,128)(2,1)}) custom-call(bf16[3072,768]{1,0:T(8,128)(2,1)} %x_ref.6, bf16[768,512]{1,0:T(8,128)(2,1)} %w_ref.2), custom_call_target="tpu_custom_call" | custom-call | flops 2415919104 | bytes 17301504 | tf_op jit(solution)/shard_map/image_head/pallas_call | solution.py:57
  21.4 0.0 collective-permute-done.txt_ref
  21.4 42.2 %away_tile.1 = (f32[3072,512]{1,0:T(8,128)}, f32[6,512,512]{2,1,0:T(8,128)}, f32[3,16,256]{2,1,0:T(8,128)}) custom-call(f32[2]{0:T(128)} %pad_maximum_fusion.1.sc_ref, bf16[3072,512]{1,0:T(8,128)(2,1)} %get-tuple-element.16.img_ref, bf16[512,3072]{1,0:T(8,128)(2,1)} %get-tuple-element.17.imgt_ref, bf16[6,512,512]{2,1,0:T(8,128)(2,1)} %collective-permute-done.txt_ref), custom_call_target="tpu_custom_call" | custom-call | flops 28991029248 | bytes 47185920 | tf_op jit(solution)/shard_map/away_tile/pallas_call | solution.py:162
  63.6 0.3 collective-permute-start.1
  63.9 47.2 %home_tile.1 = (f32[6,512,512]{2,1,0:T(8,128)}, f32[768,512]{1,0:T(8,128)}, f32[3,16,256]{2,1,0:T(8,128)}) custom-call(f32[2]{0:T(128)} %pad_maximum_fusion.1.sc_ref, bf16[3072,512]{1,0:T(8,128)(2,1)} %get-tuple-element.16.img_ref, bf16[512,3072]{1,0:T(8,128)(2,1)} %get-tuple-element.17.imgt_ref, bf16[6,512,512]{2,1,0:T(8,128)(2,1)} %bitcast.30, ...), custom_call_target="tpu_custom_call" | custom-call | flops 28991029248 | bytes 62914560 | tf_op jit(solution)/shard_map/home_tile/pallas_call | solution.py:189
  111.1 0.0 collective-permute-done.1.got_ref
  111.1 13.6 %text_back.1.a_ref = f32[2,2688,128]{2,1,0:T(8,128)} custom-call(f32[2]{0:T(128)} %pad_maximum_fusion.1.sc_ref, f32[6,512,512]{2,1,0:T(8,128)} %get-tuple-element.22.own_ref, f32[6,512,512]{2,1,0:T(8,128)} %collective-permute-done.1.got_ref, f32[3072,512]{1,0:T(8,128)} %get-tuple-element.24.raw_ref, bf16[3072,512]{1,0:T(8,128)(2,1)} %x_ref.7, ...), custom_call_target="tpu_custom_call" | custom-call | flops 1610612736 | bytes 22020096 | tf_op jit(solution)/shard_map/text_back/pallas_call | solution.py:255
  124.7 0.0 copy-start
  124.7 1.8 %copy-done = f32[2,2688,128]{2,1,0:T(8,128)S(1)} copy-done((f32[2,2688,128]{2,1,0:T(8,128)S(1)}, f32[2,2688,128]{2,1,0:T(8,128)}, u32[]{:S(2)}) %copy-start) | copy-done | bytes 2752536
  126.4 37.5 %allsum.1 = f32[2,2688,128]{2,1,0:T(8,128)S(1)} custom-call(f32[2,2688,128]{2,1,0:T(8,128)S(1)} %copy-done), custom_call_target="tpu_custom_call" | custom-call | flops 1000000000 | bytes 10000000 | tf_op jit(solution)/shard_map/allsum/pallas_call | solution.py:368
  164.0 0.5 fusion
  164.5 0.1 slice.23
  164.6 0.1 slice_bitcast_fusion
  164.7 0.1 pad_maximum_fusion
  164.8 1.4 copy.17
  166.2 1.1 copy.18
  (1 shorter events, 0.0 us)
Async XLA Ops:
  8.4 13.0 %collective-permute-start = (bf16[6,512,512]{2,1,0:T(8,128)(2,1)}, bf16[6,512,512]{2,1,0:T(8,128)(2,1)}, u32[]{:S(2)}, u32[]{:S(2)}) collective-permute-start(bf16[6,512,512]{2,1,0:T(8,128)(2,1)} %bitcast.29), channel_id=1, source_target_pairs={{0,1},{1,0},{2,3},{3,2},{4,5},{5,4},{6,7},{7,6},{8,9},{9,8},{10,11... | collective-permute-start | bytes 9437192 | tf_op jit(solution)/shard_map/ppermute | solution.py:399
  63.6 47.5 %collective-permute-start.1 = (f32[6,512,512]{2,1,0:T(8,128)}, f32[6,512,512]{2,1,0:T(8,128)}, u32[]{:S(2)}, u32[]{:S(2)}) collective-permute-start(f32[6,512,512]{2,1,0:T(8,128)} %get-tuple-element.23), channel_id=1, source_target_pairs={{0,1},{1,0},{2,3},{3,2},{4,5},{5,4},{6,7},{7,6},{8,9},{9,8},{10,11... | collective-permute-start | bytes 18874376 | tf_op jit(solution)/shard_map/ppermute | solution.py:402
  124.7 1.8 %copy-start = (f32[2,2688,128]{2,1,0:T(8,128)S(1)}, f32[2,2688,128]{2,1,0:T(8,128)}, u32[]{:S(2)}) copy-start(f32[2,2688,128]{2,1,0:T(8,128)} %text_back.1.a_ref) | copy-start | bytes 8257540

commit v3 on v2

--- a/solution.py
+++ b/solution.py
@@ -33,27 +33,29 @@
     return pltpu.CompilerParams(dimension_semantics=("arbitrary",), vmem_limit_bytes=vmem * MIB, **kw)
 
 
+def scale_of(temp_ref):
+    return jnp.exp(jnp.full((8, 128), temp_ref[0], F32))[0, 0]
+
+
 def cost(flops, nbytes):
     return pl.CostEstimate(flops=int(flops), bytes_accessed=int(nbytes), transcendentals=0)
 
 
-def head_body(x_ref, w_ref, raw_ref, emb_ref, *maybe_t):
+def head_body(x_ref, w_ref, emb_ref, *maybe_raw):
     raw = jnp.dot(x_ref[...], w_ref[...], preferred_element_type=F32)
-    raw_ref[...] = raw
-    emb = (raw * inv_norm(raw)).astype(BF16)
-    emb_ref[...] = emb
-    if maybe_t:
-        maybe_t[0][...] = emb.T
-
-
-def head(x, w, transposed, name):
+    if maybe_raw:
+        maybe_raw[0][...] = raw
+    emb_ref[...] = (raw * inv_norm(raw)).astype(BF16)
+
+
+def head(x, w, keep_raw, name):
     rows, feat = x.shape
     dim = w.shape[1]
-    out_shape = [jax.ShapeDtypeStruct((rows, dim), F32), jax.ShapeDtypeStruct((rows, dim), BF16)]
-    out_specs = [pl.BlockSpec((BM, dim), lambda i: (i, 0)), pl.BlockSpec((BM, dim), lambda i: (i, 0))]
-    if transposed:
-        out_shape.append(jax.ShapeDtypeStruct((dim, rows), BF16))
-        out_specs.append(pl.BlockSpec((dim, BM), lambda i: (0, i)))
+    out_shape = [jax.ShapeDtypeStruct((rows, dim), BF16)]
+    out_specs = [pl.BlockSpec((BM, dim), lambda i: (i, 0))]
+    if keep_raw:
+        out_shape.append(jax.ShapeDtypeStruct((rows, dim), F32))
+        out_specs.append(pl.BlockSpec((BM, dim), lambda i: (i, 0)))
     return pl.pallas_call(
         head_body,
         grid=(rows // BM,),
@@ -61,17 +63,18 @@
         out_specs=out_specs,
         out_shape=out_shape,
         compiler_params=params(62),
-        cost_estimate=cost(2 * rows * feat * dim, rows * (2 * feat + 8 * dim)),
+        cost_estimate=cost(2 * rows * feat * dim, rows * (2 * feat + 6 * dim)),
         name=name,
     )(x, w)
 
 
-def pair_terms(sc_ref, img_ref, imgt_ref, txt_ref, di_ref, dt_ref, acc, s_scr, h_scr, total_rows, home, di_init):
+def pair_terms(temp_ref, bias_ref, img_ref, txt_ref, di_ref, dt_ref, acc, s_scr, h_scr, imgt_scr, total_rows, home, di_init):
     step = pl.program_id(0)
     blocks = txt_ref.shape[0]
-    s = sc_ref[0]
-    a, b, hs = s * LOG2E, sc_ref[1] * LOG2E, s / total_rows
-    img, imgt = img_ref[...], imgt_ref[...]
+    s = scale_of(temp_ref)
+    a, b, hs = s * LOG2E, bias_ref[0] * LOG2E, s * (1.0 / total_rows)
+    img = img_ref[...]
+    imgt_scr[...] = img.T
 
     def block_of(k):
         return lax.rem(step + k, blocks) if home else k
@@ -110,7 +113,7 @@
             di_ref[...] = part if di_init is None else di_init[...] + part
         else:
             di_ref[...] += part
-        dt_ref[block_of(k)] += jnp.dot(imgt, h, preferred_element_type=F32)
+        dt_ref[block_of(k)] += jnp.dot(imgt_scr[...], h, preferred_element_type=F32)
 
     logits(0)
     for k in range(blocks):
@@ -120,23 +123,23 @@
         grads(k)
 
 
-def away_body(sc_ref, img_ref, imgt_ref, txt_ref, di_ref, dt_ref, sums_ref, s_scr, h_scr, *, total_rows):
+def away_body(temp_ref, bias_ref, img_ref, txt_ref, di_ref, dt_ref, sums_ref, s_scr, h_scr, imgt_scr, *, total_rows):
     @pl.when(pl.program_id(0) == 0)
     def _():
         sums_ref[...] = jnp.zeros_like(sums_ref)
         dt_ref[...] = jnp.zeros_like(dt_ref)
 
-    pair_terms(sc_ref, img_ref, imgt_ref, txt_ref, di_ref, dt_ref, sums_ref, s_scr, h_scr, total_rows, False, None)
-
-
-def home_body(sc_ref, img_ref, imgt_ref, txt_ref, raw_ref, x_ref, away_ref, sums_in, dt_ref, dw_ref, sums_ref, s_scr, h_scr, di_ref, *, total_rows):
+    pair_terms(temp_ref, bias_ref, img_ref, txt_ref, di_ref, dt_ref, sums_ref, s_scr, h_scr, imgt_scr, total_rows, False, None)
+
+
+def home_body(temp_ref, bias_ref, img_ref, txt_ref, raw_ref, x_ref, away_ref, sums_in, dt_ref, dw_ref, sums_ref, s_scr, h_scr, imgt_scr, di_ref, *, total_rows):
     @pl.when(pl.program_id(0) == 0)
     def _():
         sums_ref[...] = sums_in[...]
         dt_ref[...] = jnp.zeros_like(dt_ref)
         dw_ref[...] = jnp.zeros_like(dw_ref)
 
-    pair_terms(sc_ref, img_ref, imgt_ref, txt_ref, di_ref, dt_ref, sums_ref, s_scr, h_scr, total_rows, True, away_ref)
+    pair_terms(temp_ref, bias_ref, img_ref, txt_ref, di_ref, dt_ref, sums_ref, s_scr, h_scr, imgt_scr, total_rows, True, away_ref)
     dw_ref[...] += lax.dot_general(x_ref[...], raw_grad(raw_ref[...], di_ref[...]), TN, preferred_element_type=F32)
 
 
@@ -147,15 +150,15 @@
     return (inv * (grad_unit - unit * proj)).astype(BF16)
 
 
-def tile_scratch():
-    return [pltpu.VMEM((2, BM, BN), F32), pltpu.VMEM((2, BM, BN), BF16)]
+def tile_scratch(dim):
+    return [pltpu.VMEM((2, BM, BN), F32), pltpu.VMEM((2, BM, BN), BF16), pltpu.VMEM((dim, BM), BF16)]
 
 
 def whole(shape, **kw):
     return pl.BlockSpec(shape, lambda i: (0,) * len(shape), **kw)
 
 
-def away_tile(scal, img, imgt, txt, total_rows):
+def away_tile(temp, bias, img, txt, total_rows):
     rows, dim = img.shape
     blocks = txt.shape[0]
     once = dict(pipeline_mode=pl.Buffered(1))
@@ -164,8 +167,8 @@
         grid=(rows // BM,),
         in_specs=[
             pl.BlockSpec(memory_space=pltpu.SMEM),
+            pl.BlockSpec(memory_space=pltpu.SMEM),
             pl.BlockSpec((BM, dim), lambda i: (i, 0)),
-            pl.BlockSpec((dim, BM), lambda i: (0, i)),
             whole((blocks, BN, dim), **once),
         ],
         out_specs=[pl.BlockSpec((BM, dim), lambda i: (i, 0)), whole((blocks, dim, BN), **once), whole((3, CR, CC))],
@@ -174,14 +177,14 @@
             jax.ShapeDtypeStruct((blocks, dim, BN), F32),
             jax.ShapeDtypeStruct((3, CR, CC), F32),
         ],
-        scratch_shapes=tile_scratch(),
+        scratch_shapes=tile_scratch(dim),
         compiler_params=params(62),
         cost_estimate=cost(6 * rows * rows * dim, 30 * rows * dim),
         name="away_tile",
-    )(scal, img, imgt, txt)
-
-
-def home_tile(scal, img, imgt, txt, raw, x, away, sums, total_rows):
+    )(temp, bias, img, txt)
+
+
+def home_tile(temp, bias, img, txt, raw, x, away, sums, total_rows):
     rows, dim = img.shape
     feat = x.shape[1]
     blocks = txt.shape[0]
@@ -191,8 +194,8 @@
         grid=(rows // BM,),
         in_specs=[
             pl.BlockSpec(memory_space=pltpu.SMEM),
+            pl.BlockSpec(memory_space=pltpu.SMEM),
             pl.BlockSpec((BM, dim), lambda i: (i, 0)),
-            pl.BlockSpec((dim, BM), lambda i: (0, i)),
             whole((blocks, BN, dim), **once),
             pl.BlockSpec((BM, dim), lambda i: (i, 0)),
             pl.BlockSpec((BM, feat), lambda i: (i, 0)),
@@ -205,31 +208,34 @@
             jax.ShapeDtypeStruct((feat, dim), F32),
             jax.ShapeDtypeStruct((3, CR, CC), F32),
         ],
-        scratch_shapes=tile_scratch() + [pltpu.VMEM((BM, dim), F32)],
+        scratch_shapes=tile_scratch(dim) + [pltpu.VMEM((BM, dim), F32)],
         compiler_params=params(62),
         cost_estimate=cost(6 * rows * rows * dim, 40 * rows * dim),
         name="home_tile",
-    )(scal, img, imgt, txt, raw, x, away, sums)
-
-
-def text_body(sc_ref, own_ref, got_ref, raw_ref, x_ref, dwi_ref, sums_ref, out_ref, dw_ref, *, total_rows):
+    )(temp, bias, img, txt, raw, x, away, sums)
+
+
+def text_body(temp_ref, own_ref, got_ref, x_ref, w_ref, dwi_ref, sums_ref, out_ref, dwt_ref, wt_ref, *, total_rows):
     step = pl.program_id(0)
 
     @pl.when(step == 0)
     def _():
-        dw_ref[...] = jnp.zeros_like(dw_ref)
-
-    grad = (own_ref[0] + got_ref[0]).T
-    dw_ref[...] += lax.dot_general(x_ref[...], raw_grad(raw_ref[...], grad), TN, preferred_element_type=F32)
+        dwt_ref[...] = jnp.zeros_like(dwt_ref)
+        wt_ref[...] = w_ref[...].T
+
+    x = x_ref[...]
+    raw = lax.dot_general(wt_ref[...], x, NT, preferred_element_type=F32)
+    inv = lax.rsqrt(jnp.sum(raw * raw, axis=0, keepdims=True))
+    unit = raw * inv
+    grad = own_ref[0] + got_ref[0]
+    proj = jnp.sum(unit * grad, axis=0, keepdims=True)
+    raw_grad_t = (inv * (grad - unit * proj)).astype(BF16)
+    dwt_ref[...] += jnp.dot(raw_grad_t, x, preferred_element_type=F32)
 
     @pl.when(step == pl.num_programs(0) - 1)
     def _():
-        feat_i, feat_t = dwi_ref.shape[0], dw_ref.shape[0]
-        flat = []
-        for l in range(4):
-            flat.append((dwi_ref, l, feat_i))
-        for l in range(4):
-            flat.append((dw_ref, l, feat_t))
+        feat_i, feat_t = dwi_ref.shape[0], dwt_ref.shape[1]
+        flat = [(dwi_ref, l, feat_i) for l in range(4)] + [(dwt_ref, l, feat_t) for l in range(4)]
         pos = 0
         size = 2 * feat_i + 2 * feat_t
         for ref, l, n in flat:
@@ -237,21 +243,24 @@
             while done < n:
                 half, at = divmod(pos, size)
                 take = min(n - done, size - at)
-                out_ref[half, at:at + take, :] = ref[done:done + take, 128 * l:128 * (l + 1)]
+                if ref is dwt_ref:
+                    out_ref[half, at:at + take, :] = ref[128 * l:128 * (l + 1), done:done + take].T
+                else:
+                    out_ref[half, at:at + take, :] = ref[done:done + take, 128 * l:128 * (l + 1)]
                 done += take
                 pos += take
         out_ref[:, size:, :] = jnp.zeros((2, HALF - size, 128), F32)
-        s = sc_ref[0]
+        s = scale_of(temp_ref)
         row = lax.broadcasted_iota(jnp.int32, (8, 128), 0)
         loss = jnp.sum(sums_ref[0]) / total_rows
-        temp = jnp.sum(sums_ref[1]) * (s / total_rows)
+        temp = jnp.sum(sums_ref[1]) * (s * (1.0 / total_rows))
         bias = jnp.sum(sums_ref[2]) / total_rows
         out_ref[0, size:size + 8, :] = jnp.where(row == 0, loss, jnp.where(row == 1, temp, bias))
 
 
-def text_back(scal, own, got, raw, x, dwi, sums, total_rows):
-    rows, dim = raw.shape
-    feat = x.shape[1]
+def text_back(temp, own, got, x, w, dwi, sums, total_rows):
+    rows, feat = x.shape
+    dim = w.shape[1]
     return pl.pallas_call(
         functools.partial(text_body, total_rows=total_rows),
         grid=(rows // BN,),
@@ -259,18 +268,18 @@
             pl.BlockSpec(memory_space=pltpu.SMEM),
             pl.BlockSpec((1, dim, BN), lambda i: (i, 0, 0)),
             pl.BlockSpec((1, dim, BN), lambda i: (i, 0, 0)),
-            pl.BlockSpec((BN, dim), lambda i: (i, 0)),
             pl.BlockSpec((BN, feat), lambda i: (i, 0)),
+            whole((feat, dim)),
             whole(dwi.shape),
             whole((3, CR, CC)),
         ],
         out_specs=whole((2, HALF, 128)),
         out_shape=jax.ShapeDtypeStruct((2, HALF, 128), F32),
-        scratch_shapes=[pltpu.VMEM((feat, dim), F32)],
-        compiler_params=params(57),
-        cost_estimate=cost(2 * rows * feat * dim, rows * (2 * feat + 12 * dim)),
+        scratch_shapes=[pltpu.VMEM((dim, feat), F32), pltpu.VMEM((dim, feat), BF16)],
+        compiler_params=params(48),
+        cost_estimate=cost(4 * rows * feat * dim, rows * (2 * feat + 8 * dim)),
         name="text_back",
-    )(scal, own, got, raw, x, dwi, sums)
+    )(temp, own, got, x, w, dwi, sums)
 
 
 def allsum_body(a_ref, o_ref, d2d, r1, r2, r3, dsem, s1, v1, s2, v2, s3, v3, s4, v4, s5, v5):
@@ -393,15 +402,15 @@
         feat_t = txt_loc.shape[1]
         dim = w_img.shape[1]
         total_rows = float(rows * rep_n * data_n)
-        scal = jnp.stack([jnp.exp(log_temp), logit_bias])
-        raw_t, emb_t = head(txt_loc, w_txt, False, "text_head")
+        temp, bias = log_temp.reshape(1), logit_bias.reshape(1)
+        (emb_t,) = head(txt_loc, w_txt, False, "text_head")
         emb_t = emb_t.reshape(rows // BN, BN, dim)
         away_t = lax.ppermute(emb_t, "data", swap)
-        raw_i, emb_i, emb_it = head(img_loc, w_img, True, "image_head")
-        away_di, away_dt, sums = away_tile(scal, emb_i, emb_it, away_t, total_rows)
+        emb_i, raw_i = head(img_loc, w_img, True, "image_head")
+        away_di, away_dt, sums = away_tile(temp, bias, emb_i, away_t, total_rows)
         got_dt = lax.ppermute(away_dt, "data", swap)
-        own_dt, dwi, sums = home_tile(scal, emb_i, emb_it, emb_t, raw_i, img_loc, away_di, sums, total_rows)
-        packed = text_back(scal, own_dt, got_dt, raw_t, txt_loc, dwi, sums, total_rows)
+        own_dt, dwi, sums = home_tile(temp, bias, emb_i, emb_t, raw_i, img_loc, away_di, sums, total_rows)
+        packed = text_back(temp, own_dt, got_dt, txt_loc, w_txt, dwi, sums, total_rows)
         total = allsum(packed)
         size = 2 * (feat_i + feat_t)
         split = 4 * feat_i - size

time: 168 us -> 161 us (0.958)
  Pallas kernels: 158 us -> 152 us
    pallas_call x1, Pallas kernels: 13.6 us -> 10.1 us  [text_back(): pl.pallas_call(functools.partial(text_body, total_rows=total_rows), grid=...]
    pallas_call x2, Pallas kernels: 17.5 us -> 15.5 us  [head(): pl.pallas_call(head_body, grid=(rows // BM,), in_specs=[pl.BlockSpec((BM,...]
  transfers between devices with their start and end apart: 2 -> 2, of which waited for: 0 -> 0; matrix products, arithmetic and copies ran while one was open for 0% -> 0% of each run, Pallas kernels for 34% -> 35%
where the time goes in v3:
time: 161 us
  Pallas kernels  152 us (94%)
  local copies, waits for them, and re-layouts  5.37 us (3%)
  between operations  2.01 us (1%)
    pallas_call x1, Pallas kernels, home_tile(): pl.pallas_call(functools.partial(home_body, total_rows=total_rows), grid=...  46.9 us
    pallas_call x1, Pallas kernels, away_tile(): pl.pallas_call(functools.partial(away_body, total_rows=total_rows), grid=...  41.7 us
    pallas_call x1, Pallas kernels, allsum(): pl.pallas_call(allsum_body, in_specs=[pl.BlockSpec(memory_space=pltpu.VME...  37.7 us
    pallas_call x2, Pallas kernels, head(): pl.pallas_call(head_body, grid=(rows // BM,), in_specs=[pl.BlockSpec((BM,...  15.5 us
    pallas_call x1, Pallas kernels, text_back(): pl.pallas_call(functools.partial(text_body, total_rows=total_rows), grid=...  10.1 us
  transfers between devices with their start and end apart: 2, of which 0 were waited for; matrix products, arithmetic and copies ran while one was open for 0% of the time, Pallas kernels for 35%

profile of v3, /device:TPU:1, one launch (start us, length us, event | category | flops | bytes accessed | tf_op | source)
XLA Modules:
  0.0 160.7 jit_solution(6642832806033450359)
XLA Ops:
  0.6 6.8 %text_head.1 = bf16[3072,512]{1,0:T(8,128)(2,1)} custom-call(bf16[3072,512]{1,0:T(8,128)(2,1)} %x_ref.7, bf16[512,512]{1,0:T(8,128)(2,1)} %w_ref.5), custom_call_target="tpu_custom_call" | custom-call | flops 1610612736 | bytes 12582912 | tf_op jit(solution)/shard_map/text_head/pallas_call | solution.py:59
  7.4 1.4 collective-permute-start
  10.1 8.7 %image_head.1 = (bf16[3072,512]{1,0:T(8,128)(2,1)}, f32[3072,512]{1,0:T(8,128)}) custom-call(bf16[3072,768]{1,0:T(8,128)(2,1)} %x_ref.6, bf16[768,512]{1,0:T(8,128)(2,1)} %w_ref.3), custom_call_target="tpu_custom_call" | custom-call | flops 2415919104 | bytes 14155776 | tf_op jit(solution)/shard_map/image_head/pallas_call | solution.py:59
  18.8 0.0 collective-permute-done.txt_ref
  18.8 41.7 %away_tile.1 = (f32[3072,512]{1,0:T(8,128)}, f32[6,512,512]{2,1,0:T(8,128)}, f32[3,16,256]{2,1,0:T(8,128)}) custom-call(f32[1]{0:T(128)} %bitcast.24.temp_ref, f32[1]{0:T(128)} %bitcast.27.bias_ref, bf16[3072,512]{1,0:T(8,128)(2,1)} %get-tuple-element.13.img_ref, bf16[6,512,512]{2,1,0:T(8,128)(2,1)} %collective-permute-done.txt_ref), custom_call_target="tpu_custom_call" | custom-call | flops 28991029248 | bytes 47185920 | tf_op jit(solution)/shard_map/away_tile/pallas_call | solution.py:165
  60.5 0.0 collective-permute-start.1
  60.5 0.0 copy-start
  60.5 46.9 %home_tile.1 = (f32[6,512,512]{2,1,0:T(8,128)}, f32[768,512]{1,0:T(8,128)}, f32[3,16,256]{2,1,0:T(8,128)}) custom-call(f32[1]{0:T(128)} %bitcast.25.temp_ref, f32[1]{0:T(128)} %bitcast.28.bias_ref, bf16[3072,512]{1,0:T(8,128)(2,1)} %get-tuple-element.13.img_ref, bf16[6,512,512]{2,1,0:T(8,128)(2,1)} %bitcast.32, f32[3072,512]{1,0:T(8,128)} %get-tuple-element.14.raw_ref, ...), custom_call_target="tpu_custom_call" | custom-call | flops 28991029248 | bytes 62914560 | tf_op jit(solution)/shard_map/home_tile/pallas_call | solution.py:192
  107.4 0.0 collective-permute-done.1.got_ref
  107.4 0.0 copy-done
  107.4 0.0 copy-start.1
  107.4 1.4 copy-done.1
  108.8 0.0 copy-start.2
  108.8 0.8 copy-done.2
  109.6 10.1 %text_back.1.a_ref = f32[2,2688,128]{2,1,0:T(8,128)S(1)} custom-call(f32[1]{0:T(128)} %bitcast.26.temp_ref, f32[6,512,512]{2,1,0:T(8,128)} %get-tuple-element.17.own_ref, f32[6,512,512]{2,1,0:T(8,128)} %collective-permute-done.1.got_ref, bf16[3072,512]{1,0:T(8,128)(2,1)} %x_ref.7, bf16[512,512]{1,0:T(8,128)(2,1)S(1)} %copy-done, f32[768,512]{1,0:T(8,128)S(1)} %copy-done.1, ...), custom_call_target="tpu_custom_call" | custom-call | flops 3221225472 | bytes 15728640 | tf_op jit(solution)/shard_map/text_back/pallas_call | solution.py:264
  119.7 37.7 %allsum.1 = f32[2,2688,128]{2,1,0:T(8,128)S(1)} custom-call(f32[2,2688,128]{2,1,0:T(8,128)S(1)} %text_back.1.a_ref), custom_call_target="tpu_custom_call" | custom-call | flops 1000000000 | bytes 10000000 | tf_op jit(solution)/shard_map/allsum/pallas_call | solution.py:377
  157.4 0.5 fusion
  158.0 0.1 slice.23
  158.0 0.1 slice_bitcast_fusion
  158.1 0.1 pad_maximum_fusion
  158.2 1.4 copy.17
  159.6 1.1 copy.18
  (1 shorter events, 0.0 us)
Async XLA Ops:
  7.4 11.3 %collective-permute-start = (bf16[6,512,512]{2,1,0:T(8,128)(2,1)}, bf16[6,512,512]{2,1,0:T(8,128)(2,1)}, u32[]{:S(2)}, u32[]{:S(2)}) collective-permute-start(bf16[6,512,512]{2,1,0:T(8,128)(2,1)} %bitcast.31), channel_id=1, source_target_pairs={{0,1},{1,0},{2,3},{3,2},{4,5},{5,4},{6,7},{7,6},{8,9},{9,8},{10,11... | collective-permute-start | bytes 9437192 | tf_op jit(solution)/shard_map/ppermute | solution.py:408
  60.5 46.9 %collective-permute-start.1 = (f32[6,512,512]{2,1,0:T(8,128)}, f32[6,512,512]{2,1,0:T(8,128)}, u32[]{:S(2)}, u32[]{:S(2)}) collective-permute-start(f32[6,512,512]{2,1,0:T(8,128)} %get-tuple-element.18), channel_id=1, source_target_pairs={{0,1},{1,0},{2,3},{3,2},{4,5},{5,4},{6,7},{7,6},{8,9},{9,8},{10,11... | collective-permute-start | bytes 18874376 | tf_op jit(solution)/shard_map/ppermute | solution.py:411
  60.5 46.9 %copy-start = (bf16[512,512]{1,0:T(8,128)(2,1)S(1)}, bf16[512,512]{1,0:T(8,128)(2,1)}, u32[]{:S(2)}) copy-start(bf16[512,512]{1,0:T(8,128)(2,1)} %w_ref.5) | copy-start | bytes 1572868
  107.4 1.4 copy-start.1
  108.8 0.8 copy-start.2

commit v4 on v3

v4 whole, which is shorter than its diff:
```python
import functools

import jax
import jax.numpy as jnp
from jax import lax
from jax.experimental import pallas as pl
from jax.experimental.pallas import tpu as pltpu
from jax.sharding import PartitionSpec as P

LOG2E = 1.4426950408889634
LN2 = 0.6931471805599453
NT = (((1,), (1,)), ((), ()))
TN = (((0,), (0,)), ((), ()))
MESH = pl.DeviceIdType.MESH
F32 = jnp.float32
BF16 = jnp.bfloat16
MIB = 1024 * 1024

BM = 512
BN = 512
CR, CC = 16, 256


def inv_norm(raw):
    return lax.rsqrt(jnp.sum(raw * raw, axis=1, keepdims=True))


def params(vmem, **kw):
    return pltpu.CompilerParams(dimension_semantics=("arbitrary",), vmem_limit_bytes=vmem * MIB, **kw)


def scale_of(sc_ref):
    return jnp.exp(jnp.full((8, 128), sc_ref[0], F32))[0, 0]


def cost(flops, nbytes):
    return pl.CostEstimate(flops=int(flops), bytes_accessed=int(nbytes), transcendentals=0)


def fetch(pairs, sems):
    copies = [pltpu.make_async_copy(src, dst, sems.at[i]) for i, (src, dst) in enumerate(pairs)]
    for copy in copies:
        copy.start()
    return copies


def head_body(x_hbm, w_hbm, *refs, keep_raw):
    outs, (x_ref, w_ref, emb_ref, raw_ref, in_sem, out_sem) = refs[:-6], refs[-6:]
    blocks = x_ref.shape[0]
    arrive = fetch([(w_hbm, w_ref)] + [(x_hbm.at[pl.ds(BM * i, BM)], x_ref.at[i]) for i in range(blocks)], in_sem)
    arrive[0].wait()
    leave = []
    for i in range(blocks):
        arrive[i + 1].wait()
        raw = jnp.dot(x_ref[i], w_ref[...], preferred_element_type=F32)
        emb_ref[i] = (raw * inv_norm(raw)).astype(BF16)
        pairs = [(emb_ref.at[i], outs[0].at[pl.ds(BM * i, BM)])]
        if keep_raw:
            raw_ref[i] = raw
            pairs.append((raw_ref.at[i], outs[1].at[pl.ds(BM * i, BM)]))
        leave += fetch(pairs, out_sem.at[i])
    for copy in leave:
        copy.wait()


def head(x, w, keep_raw, name):
    rows, feat = x.shape
    dim = w.shape[1]
    blocks = rows // BM
    hbm = pl.BlockSpec(memory_space=pl.ANY)
    out_shape = [jax.ShapeDtypeStruct((rows, dim), BF16)]
    if keep_raw:
        out_shape.append(jax.ShapeDtypeStruct((rows, dim), F32))
    return pl.pallas_call(
        functools.partial(head_body, keep_raw=keep_raw),
        in_specs=[hbm, hbm],
        out_specs=[hbm] * len(out_shape),
        out_shape=out_shape,
        scratch_shapes=[
            pltpu.VMEM((blocks, BM, feat), BF16),
            pltpu.VMEM((feat, dim), BF16),
            pltpu.VMEM((blocks, BM, dim), BF16),
            pltpu.VMEM((blocks if keep_raw else 1, BM, dim), F32),
            pltpu.SemaphoreType.DMA((blocks + 1,)),
            pltpu.SemaphoreType.DMA((blocks, 2)),
        ],
        compiler_params=pltpu.CompilerParams(vmem_limit_bytes=62 * MIB),
        cost_estimate=cost(2 * rows * feat * dim, rows * (2 * feat + 6 * dim)),
        name=name,
    )(x, w)


def pair_terms(sc_ref, img_ref, txt_ref, di_ref, dt_ref, acc, s_scr, h_scr, imgt_scr, total_rows, home, di_init):
    step = pl.program_id(0)
    blocks = txt_ref.shape[0]
    s = scale_of(sc_ref)
    a, b, hs = s * LOG2E, sc_ref[1] * LOG2E, s * (1.0 / total_rows)
    img = img_ref[...]
    imgt_scr[...] = img.T

    def block_of(k):
        return lax.rem(step + k, blocks) if home else k

    def logits(k):
        s_scr[k % 2] = lax.dot_general(img, txt_ref[block_of(k)], NT, preferred_element_type=F32)

    def terms(k):
        zero = jnp.zeros((CR, CC), F32)
        top, prod, g_sum, gs_sum = zero, zero, zero, zero
        for r in range(0, BM, CR):
            for c in range(0, BN, CC):
                dots = s_scr[k % 2, r:r + CR, c:c + CC]
                z = dots * a + b
                pos = jnp.maximum(z, 0.0)
                t = jnp.exp2(-jnp.abs(z))
                rcp = 1.0 / (1.0 + t)
                sig = jnp.where(z >= 0, rcp, t * rcp)
                if home and k == 0 and r < c + CC and c < r + CR:
                    eye = (lax.broadcasted_iota(jnp.int32, (CR, CC), 0) + r) == (lax.broadcasted_iota(jnp.int32, (CR, CC), 1) + c)
                    sig = jnp.where(eye, -jnp.where(z >= 0, t * rcp, rcp), sig)
                    pos = jnp.where(eye, jnp.maximum(-z, 0.0), pos)
                top = top + pos
                prod = (prod + t) + prod * t
                g_sum = g_sum + sig
                gs_sum = gs_sum + sig * dots
                h_scr[k % 2, r:r + CR, c:c + CC] = (sig * hs).astype(BF16)
        acc[0] += LN2 * top + jnp.log1p(prod)
        acc[1] += gs_sum
        acc[2] += g_sum

    def grads(k):
        h = h_scr[k % 2]
        part = jnp.dot(h, txt_ref[block_of(k)], preferred_element_type=F32)
        if k == 0:
            di_ref[...] = part if di_init is None else di_init[...] + part
        else:
            di_ref[...] += part
        dt_ref[block_of(k)] += jnp.dot(imgt_scr[...], h, preferred_element_type=F32)

    logits(0)
    for k in range(blocks):
        if k + 1 < blocks:
            logits(k + 1)
        terms(k)
        grads(k)


def away_body(sc_ref, img_ref, txt_ref, di_ref, dt_ref, sums_ref, s_scr, h_scr, imgt_scr, *, total_rows):
    @pl.when(pl.program_id(0) == 0)
    def _():
        sums_ref[...] = jnp.zeros_like(sums_ref)
        dt_ref[...] = jnp.zeros_like(dt_ref)

    pair_terms(sc_ref, img_ref, txt_ref, di_ref, dt_ref, sums_ref, s_scr, h_scr, imgt_scr, total_rows, False, None)


def home_body(sc_ref, img_ref, txt_ref, raw_ref, x_ref, away_ref, sums_in, dt_ref, dw_ref, sums_ref, s_scr, h_scr, imgt_scr, di_ref, *, total_rows):
    @pl.when(pl.program_id(0) == 0)
    def _():
        sums_ref[...] = sums_in[...]
        dt_ref[...] = jnp.zeros_like(dt_ref)
        dw_ref[...] = jnp.zeros_like(dw_ref)

    pair_terms(sc_ref, img_ref, txt_ref, di_ref, dt_ref, sums_ref, s_scr, h_scr, imgt_scr, total_rows, True, away_ref)
    dw_ref[...] += lax.dot_general(x_ref[...], raw_grad(raw_ref[...], di_ref[...]), TN, preferred_element_type=F32)


def raw_grad(raw, grad_unit):
    inv = inv_norm(raw)
    unit = raw * inv
    proj = jnp.sum(unit * grad_unit, axis=1, keepdims=True)
    return (inv * (grad_unit - unit * proj)).astype(BF16)


def tile_scratch(dim):
    return [pltpu.VMEM((2, BM, BN), F32), pltpu.VMEM((2, BM, BN), BF16), pltpu.VMEM((dim, BM), BF16)]


def whole(shape, **kw):
    return pl.BlockSpec(shape, lambda i: (0,) * len(shape), **kw)


def away_tile(scal, img, txt, total_rows):
    rows, dim = img.shape
    blocks = txt.shape[0]
    once = dict(pipeline_mode=pl.Buffered(1))
    return pl.pallas_call(
        functools.partial(away_body, total_rows=total_rows),
        grid=(rows // BM,),
        in_specs=[
            pl.BlockSpec(memory_space=pltpu.SMEM),
            pl.BlockSpec((BM, dim), lambda i: (i, 0)),
            whole((blocks, BN, dim), **once),
        ],
        out_specs=[pl.BlockSpec((BM, dim), lambda i: (i, 0)), whole((blocks, dim, BN), **once), whole((3, CR, CC))],
        out_shape=[
            jax.ShapeDtypeStruct((rows, dim), F32),
            jax.ShapeDtypeStruct((blocks, dim, BN), F32),
            jax.ShapeDtypeStruct((3, CR, CC), F32),
        ],
        scratch_shapes=tile_scratch(dim),
        compiler_params=params(62),
        cost_estimate=cost(6 * rows * rows * dim, 30 * rows * dim),
        name="away_tile",
    )(scal, img, txt)


def home_tile(scal, img, txt, raw, x, away, sums, total_rows):
    rows, dim = img.shape
    feat = x.shape[1]
    blocks = txt.shape[0]
    once = dict(pipeline_mode=pl.Buffered(1))
    return pl.pallas_call(
        functools.partial(home_body, total_rows=total_rows),
        grid=(rows // BM,),
        in_specs=[
            pl.BlockSpec(memory_space=pltpu.SMEM),
            pl.BlockSpec((BM, dim), lambda i: (i, 0)),
            whole((blocks, BN, dim), **once),
            pl.BlockSpec((BM, dim), lambda i: (i, 0)),
            pl.BlockSpec((BM, feat), lambda i: (i, 0)),
            pl.BlockSpec((BM, dim), lambda i: (i, 0)),
            whole((3, CR, CC)),
        ],
        out_specs=[whole((blocks, dim, BN), **once), whole((feat, dim), **once), whole((3, CR, CC))],
        out_shape=[
            jax.ShapeDtypeStruct((blocks, dim, BN), F32),
            jax.ShapeDtypeStruct((feat, dim), F32),
            jax.ShapeDtypeStruct((3, CR, CC), F32),
        ],
        scratch_shapes=tile_scratch(dim) + [pltpu.VMEM((BM, dim), F32)],
        compiler_params=params(62),
        cost_estimate=cost(6 * rows * rows * dim, 40 * rows * dim),
        name="home_tile",
    )(scal, img, txt, raw, x, away, sums)


def all_sum(src, out, bufs, peer, coord, core, send):
    pair, r1, r2, r3, psem, ssem, rsem = bufs
    part = src.shape[1] // 3
    quart, sixt = part // 4, part // 16
    sib = peer(3, 1)
    mine = out.at[core]
    dims = [(p, (p + 1) % 3, (p + 2) % 3) for p in range(3)]
    offs = (2, 1, 3)

    def spread(phase, p, d, src_of, dst_of):
        return [send(src_of(o), dst_of(o), ssem.at[phase, p, o - 1], rsem.at[phase, p, o - 1], peer(d, o)) for o in offs]

    c0 = []
    for p in range(3):
        rows = pl.ds(part * p, part)
        c0.append(send(src.at[1 - core, rows], pair.at[rows], psem.at[0, p], psem.at[1, p], sib))
    yield
    c1 = []
    for p in range(3):
        c0[p].wait_recv()
        rows = pl.ds(part * p, part)
        pair[rows, :] = pair[rows, :] + src[core, rows, :]
        d = dims[p][0]
        c1.append(spread(0, p, d, lambda o: pair.at[pl.ds(part * p + lax.rem(coord[d] + o, 4) * quart, quart)], lambda o: r1.at[p, o - 1]))
    yield
    c2, base1 = [], []
    for p in range(3):
        for copy in c1[p]:
            copy.wait_recv()
        base = part * p + coord[dims[p][0]] * quart
        base1.append(base)
        rows = pl.ds(base, quart)
        pair[rows, :] = ((pair[rows, :] + r1[p, 0]) + r1[p, 1]) + r1[p, 2]
        d = dims[p][1]
        c2.append(spread(1, p, d, lambda o: pair.at[pl.ds(base + lax.rem(coord[d] + o, 4) * sixt, sixt)], lambda o: r2.at[p, o - 1]))
    yield
    c3, base2 = [], []
    for p in range(3):
        for copy in c2[p]:
            copy.wait_recv()
        base = base1[p] + coord[dims[p][1]] * sixt
        base2.append(base)
        d = dims[p][2]
        k = coord[d]
        r3[p, k] = ((pair[pl.ds(base, sixt), :] + r2[p, 0]) + r2[p, 1]) + r2[p, 2]
        c3.append(spread(2, p, d, lambda o: r3.at[p, k], lambda o: r3.at[p, k]))
    yield
    c4 = []
    for p in range(3):
        for copy in c3[p]:
            copy.wait_recv()
        rows = pl.ds(base2[p], sixt)
        out[core, rows, :] = ((r3[p, 0] + r3[p, 1]) + r3[p, 2]) + r3[p, 3]
        c4.append(spread(3, p, dims[p][1], lambda o: mine.at[rows], lambda o: mine.at[rows]))
    yield
    c5, c6 = [], []
    for p in range(3):
        for copy in c4[p]:
            copy.wait_recv()
        rows = pl.ds(base1[p], quart)
        c5.append(spread(4, p, dims[p][0], lambda o: mine.at[rows], lambda o: mine.at[rows]))
        c6.append(send(mine.at[rows], mine.at[rows], psem.at[2, p], psem.at[3, p], sib))
    yield
    for p in range(3):
        for i, o in enumerate(offs):
            c5[p][i].wait_recv()
            rows = pl.ds(part * p + lax.rem(coord[dims[p][0]] + 4 - o, 4) * quart, quart)
            c6.append(send(mine.at[rows], mine.at[rows], psem.at[4 + 2 * i, p], psem.at[5 + 2 * i, p], sib))
    yield
    for copy in c6:
        copy.wait_recv()
    yield


def sum_scratch(rows):
    part = rows // 3
    dma = pltpu.SemaphoreType.DMA
    return [
        pltpu.VMEM((rows, 128), F32),
        pltpu.VMEM((3, 3, part // 4, 128), F32),
        pltpu.VMEM((3, 3, part // 16, 128), F32),
        pltpu.VMEM((3, 4, part // 16, 128), F32),
        dma((10, 3)),
        dma((5, 3, 3)),
        dma((5, 3, 3)),
    ]


def finish_body(sc_ref, own_hbm, got_hbm, x_hbm, w_hbm, dwi_hbm, sums_hbm, oi_ref, ot_ref, own_ref, got_ref, x_ref, w_ref, dwi_ref, sums_ref, dwt_ref, ai_ref, at_ref, sem, *bufs, total_rows):
    rep, core = lax.axis_index("rep"), lax.axis_index("data")
    coord = [lax.rem(rep, 4), lax.rem(lax.div(rep, 4), 4), lax.div(rep, 16)]
    stride = [1, 4, 16]

    def peer(dim, off):
        if dim == 3:
            return (rep, 1 - core)
        return (rep + (lax.rem(coord[dim] + off, 4) - coord[dim]) * stride[dim], core)

    bar = pltpu.get_barrier_semaphore()
    partners = [peer(3, 1)] + [peer(dim, off) for dim in range(3) for off in (1, 2, 3)]
    for dev in partners:
        pl.semaphore_signal(bar, inc=1, device_id=dev, device_id_type=MESH)

    blocks = own_ref.shape[0]
    pairs = [(dwi_hbm, dwi_ref), (w_hbm, w_ref)]
    for i in range(blocks):
        pairs += [(x_hbm.at[pl.ds(BN * i, BN)], x_ref.at[i]), (own_hbm.at[i], own_ref.at[i]), (got_hbm.at[i], got_ref.at[i])]
    arrive = fetch(pairs + [(sums_hbm, sums_ref)], sem)

    feat_i, feat_t = dwi_ref.shape[0], dwt_ref.shape[1]
    arrive[0].wait()
    for l in range(4):
        ai_ref[l // 2, pl.ds(feat_i * (l % 2), feat_i), :] = dwi_ref[:, 128 * l:128 * (l + 1)]
    pl.semaphore_wait(bar, len(partners))

    started = []

    def send(src, dst, ssem, rsem, dev):
        copy = pltpu.make_async_remote_copy(src_ref=src, dst_ref=dst, send_sem=ssem, recv_sem=rsem, device_id=dev, device_id_type=MESH)
        copy.start()
        started.append(copy)
        return copy

    img = all_sum(ai_ref, oi_ref, bufs[:7], peer, coord, core, send)
    txt = all_sum(at_ref, ot_ref, bufs[7:], peer, coord, core, send)
    next(img)
    arrive[1].wait()
    w_t = w_ref[...].T

    def block(i):
        for copy in arrive[2 + 3 * i:5 + 3 * i]:
            copy.wait()
        x = x_ref[i]
        raw = lax.dot_general(w_t, x, NT, preferred_element_type=F32)
        inv = lax.rsqrt(jnp.sum(raw * raw, axis=0, keepdims=True))
        unit = raw * inv
        grad = own_ref[i] + got_ref[i]
        proj = jnp.sum(unit * grad, axis=0, keepdims=True)
        raw_grad_t = (inv * (grad - unit * proj)).astype(BF16)
        part = jnp.dot(raw_grad_t, x, preferred_element_type=F32)
        dwt_ref[...] = part if i == 0 else dwt_ref[...] + part

    for i in range(blocks):
        block(i)
        if i == 1:
            next(img)
    for l in range(4):
        at_ref[l // 2, pl.ds(feat_t * (l % 2), feat_t), :] = dwt_ref[128 * l:128 * (l + 1), :].T
    arrive[-1].wait()
    s = scale_of(sc_ref)
    row = lax.broadcasted_iota(jnp.int32, (128, 128), 0)
    loss = jnp.sum(sums_ref[0]) / total_rows
    temp = jnp.sum(sums_ref[1]) * (s * (1.0 / total_rows))
    bias = jnp.sum(sums_ref[2]) / total_rows
    scalars = jnp.where(row == 0, loss, jnp.where(row == 1, temp, jnp.where(row == 2, bias, 0.0)))
    at_ref[0, 2 * feat_t:, :] = scalars
    at_ref[1, 2 * feat_t:, :] = jnp.zeros_like(scalars)
    next(txt)
    next(img)
    for _ in range(6):
        next(txt, None)
        next(img, None)
    next(txt, None)
    for copy in started:
        copy.wait_send()


def finish(scal, own, got, x, w, dwi, sums, total_rows):
    rows, feat = x.shape
    dim = w.shape[1]
    blocks = rows // BN
    img_rows, txt_rows = 2 * dwi.shape[0], 2 * feat + 128
    hbm = pl.BlockSpec(memory_space=pl.ANY)
    vmem = pl.BlockSpec(memory_space=pltpu.VMEM)
    return pl.pallas_call(
        functools.partial(finish_body, total_rows=total_rows),
        in_specs=[pl.BlockSpec(memory_space=pltpu.SMEM)] + [hbm] * 6,
        out_specs=[vmem, vmem],
        out_shape=[jax.ShapeDtypeStruct((2, img_rows, 128), F32), jax.ShapeDtypeStruct((2, txt_rows, 128), F32)],
        scratch_shapes=[
            pltpu.VMEM(own.shape, F32),
            pltpu.VMEM(own.shape, F32),
            pltpu.VMEM((blocks, BN, feat), BF16),
            pltpu.VMEM(w.shape, BF16),
            pltpu.VMEM(dwi.shape, F32),
            pltpu.VMEM(sums.shape, F32),
            pltpu.VMEM((dim, feat), F32),
            pltpu.VMEM((2, img_rows, 128), F32),
            pltpu.VMEM((2, txt_rows, 128), F32),
            pltpu.SemaphoreType.DMA((3 * blocks + 3,)),
        ] + sum_scratch(img_rows) + sum_scratch(txt_rows),
        compiler_params=pltpu.CompilerParams(collective_id=1, has_side_effects=True, vmem_limit_bytes=62 * MIB),
        cost_estimate=cost(1e9, 1e7),
        name="finish",
    )(scal, own, got, x, w, dwi, sums)


def solution(mesh):
    data_n, rep_n = mesh.shape["data"], mesh.shape["rep"]
    swap = [(src, (src + 1) % data_n) for src in range(data_n)]
    row_spec = P(("rep", "data"), None)

    def device_body(img_loc, txt_loc, w_img, w_txt, log_temp, logit_bias):
        rows, feat_i = img_loc.shape
        feat_t = txt_loc.shape[1]
        dim = w_img.shape[1]
        total_rows = float(rows * rep_n * data_n)
        scal = jnp.where(jnp.arange(2) == 0, log_temp, logit_bias)
        (emb_t,) = head(txt_loc, w_txt, False, "text_head")
        emb_t = emb_t.reshape(rows // BN, BN, dim)
        away_t = lax.ppermute(emb_t, "data", swap)
        emb_i, raw_i = head(img_loc, w_img, True, "image_head")
        away_di, away_dt, sums = away_tile(scal, emb_i, away_t, total_rows)
        got_dt = lax.ppermute(away_dt, "data", swap)
        own_dt, dwi, sums = home_tile(scal, emb_i, emb_t, raw_i, img_loc, away_di, sums, total_rows)
        img_sum, txt_sum = finish(scal, own_dt, got_dt, txt_loc, w_txt, dwi, sums, total_rows)
        dw_img = img_sum.reshape(4, feat_i, 128).transpose(1, 0, 2).reshape(feat_i, dim)
        dw_txt = txt_sum[:, :2 * feat_t].reshape(4, feat_t, 128).transpose(1, 0, 2).reshape(feat_t, dim)
        scalars = txt_sum[0, 2 * feat_t:2 * feat_t + 3, 0]
        return scalars[0], scalars[1], scalars[2], dw_img, dw_txt

    return jax.shard_map(device_body, mesh=mesh, in_specs=(row_spec, row_spec, P(), P(), P(), P()), out_specs=(P(), P(), P(), P(), P()), check_vma=False)
```

time: 161 us -> 152 us (0.944)
  Pallas kernels: 152 us -> 143 us
    pallas_call x4 -> x3, Pallas kernels: 63.3 us -> 53.9 us  [the longest x1 41.8 us: finish(): pl.pallas_call(functools.partial(finish_body, total_rows=total_rows), in_...]
    unnamed x6 -> x2, local copies, waits for them, and re-layouts: 2.21 us -> 0.01 us
    slice x2, local copies, waits for them, and re-layouts: 0.59 us -> 2.62 us  [the longest x1 1.33 us: device_body(): return (scalars[0], scalars[1], scalars[2], dw_img, dw_txt)]
where the time goes in v4:
time: 152 us
  Pallas kernels  143 us (94%)
  local copies, waits for them, and re-layouts  5.1 us (3%)
  between operations  1.99 us (1%)
    pallas_call x1, Pallas kernels, home_tile(): pl.pallas_call(functools.partial(home_body, total_rows=total_rows), grid=...  46.9 us
    pallas_call x1, Pallas kernels, away_tile(): pl.pallas_call(functools.partial(away_body, total_rows=total_rows), grid=...  41.9 us
    pallas_call x1, Pallas kernels, finish(): pl.pallas_call(functools.partial(finish_body, total_rows=total_rows), in_...  41.8 us
    pallas_call x2, Pallas kernels, head(): pl.pallas_call(functools.partial(head_body, keep_raw=keep_raw), in_specs=...  12 us
  transfers between devices with their start and end apart: 2, of which 0 were waited for; matrix products, arithmetic and copies ran while one was open for 0% of the time, Pallas kernels for 35%

profile of v4, /device:TPU:1, one launch (start us, length us, event | category | flops | bytes accessed | tf_op | source)
XLA Modules:
  0.0 151.8 jit_solution(9499910105205350779)
XLA Ops:
  0.6 5.3 %text_head.1 = bf16[3072,512]{1,0:T(8,128)(2,1)} custom-call(bf16[3072,512]{1,0:T(8,128)(2,1)} %x_hbm.5, bf16[512,512]{1,0:T(8,128)(2,1)} %w_hbm.5), custom_call_target="tpu_custom_call" | custom-call | flops 1610612736 | bytes 12582912 | tf_op jit(solution)/shard_map/text_head/pallas_call | solution.py:74
  6.0 1.4 collective-permute-start
  8.7 0.5 compare_select_fusion.sc_ref
  9.2 6.7 %image_head.1 = (bf16[3072,512]{1,0:T(8,128)(2,1)}, f32[3072,512]{1,0:T(8,128)}) custom-call(bf16[3072,768]{1,0:T(8,128)(2,1)} %x_ref.1, bf16[768,512]{1,0:T(8,128)(2,1)} %w_hbm.3), custom_call_target="tpu_custom_call" | custom-call | flops 2415919104 | bytes 14155776 | tf_op jit(solution)/shard_map/image_head/pallas_call | solution.py:74
  15.9 0.0 collective-permute-done.txt_ref
  15.9 41.9 %away_tile.1 = (f32[3072,512]{1,0:T(8,128)}, f32[6,512,512]{2,1,0:T(8,128)}, f32[3,16,256]{2,1,0:T(8,128)}) custom-call(f32[2]{0:T(128)} %compare_select_fusion.sc_ref, bf16[3072,512]{1,0:T(8,128)(2,1)} %get-tuple-element.15.img_ref, bf16[6,512,512]{2,1,0:T(8,128)(2,1)} %collective-permute-done.txt_ref), custom_call_target="tpu_custom_call" | custom-call | flops 28991029248 | bytes 47185920 | tf_op jit(solution)/shard_map/away_tile/pallas_call | solution.py:187
  57.9 0.0 collective-permute-start.1
  57.9 46.9 %home_tile.1 = (f32[6,512,512]{2,1,0:T(8,128)}, f32[768,512]{1,0:T(8,128)}, f32[3,16,256]{2,1,0:T(8,128)}) custom-call(f32[2]{0:T(128)} %compare_select_fusion.sc_ref, bf16[3072,512]{1,0:T(8,128)(2,1)} %get-tuple-element.15.img_ref, bf16[6,512,512]{2,1,0:T(8,128)(2,1)} %bitcast.20, f32[3072,512]{1,0:T(8,128)} %get-tuple-element.16.raw_ref, ...), custom_call_target="tpu_custom_call" | custom-call | flops 28991029248 | bytes 62914560 | tf_op jit(solution)/shard_map/home_tile/pallas_call | solution.py:213
  104.8 0.0 collective-permute-done.1.got_hbm
  104.8 41.8 %finish.1 = (f32[2,1536,128]{2,1,0:T(8,128)}, f32[2,1152,128]{2,1,0:T(8,128)}) custom-call(f32[2]{0:T(128)} %compare_select_fusion.sc_ref, f32[6,512,512]{2,1,0:T(8,128)} %get-tuple-element.19.own_hbm, f32[6,512,512]{2,1,0:T(8,128)} %collective-permute-done.1.got_hbm, bf16[3072,512]{1,0:T(8,128)(2,1)} %x_hbm.5, bf16[512,512]{1,0:T(8,128)(2,1)} %w_hbm.5, ...), custom_call_target="tpu_custom_call" | custom-call | flops 1000000000 | bytes 10000000 | tf_op jit(solution)/shard_map/finish/pallas_call | solution.py:412
  146.6 0.0 copy-start
  146.7 1.3 fusion
  148.0 1.3 slice.22
  149.3 0.0 copy-done
  149.3 1.4 copy.17
  150.7 1.1 copy.18
Async XLA Ops:
  6.0 10.0 %collective-permute-start = (bf16[6,512,512]{2,1,0:T(8,128)(2,1)}, bf16[6,512,512]{2,1,0:T(8,128)(2,1)}, u32[]{:S(2)}, u32[]{:S(2)}) collective-permute-start(bf16[6,512,512]{2,1,0:T(8,128)(2,1)} %bitcast.19), channel_id=1, source_target_pairs={{0,1},{1,0},{2,3},{3,2},{4,5},{5,4},{6,7},{7,6},{8,9},{9,8},{10,11... | collective-permute-start | bytes 9437192 | tf_op jit(solution)/shard_map/ppermute | solution.py:448
  57.9 47.0 %collective-permute-start.1 = (f32[6,512,512]{2,1,0:T(8,128)}, f32[6,512,512]{2,1,0:T(8,128)}, u32[]{:S(2)}, u32[]{:S(2)}) collective-permute-start(f32[6,512,512]{2,1,0:T(8,128)} %get-tuple-element.20), channel_id=1, source_target_pairs={{0,1},{1,0},{2,3},{3,2},{4,5},{5,4},{6,7},{7,6},{8,9},{9,8},{10,11... | collective-permute-start | bytes 18874376 | tf_op jit(solution)/shard_map/ppermute | solution.py:451
  146.6 2.6 %copy-start = (f32[2,1536,128]{2,1,0:T(8,128)S(1)}, f32[2,1536,128]{2,1,0:T(8,128)}, u32[]{:S(2)}) copy-start(f32[2,1536,128]{2,1,0:T(8,128)} %get-tuple-element.24) | copy-start | bytes 4718596
